TPU v7x, 256 devices: a whole 4x4x8 slice. The times are simulated.
256 devices in a mesh: tx: 64 (over z, y, x_hi), ty: 2 (over x_lo), mem: 2 (over core).
Axes of the slice: x: 4 (x_hi: 2, x_lo: 2; x = x_hi * 2 + x_lo), y: 4, z: 8, core: 2. Of those that a mesh axis runs over, the one named last changes fastest.
Arguments:
- obs_value: float32 [2097152], P(('tx', 'ty', 'mem')), may hold values from -6 to 6
- obs_frac: float32 [2, 2097152], P(None, ('tx', 'ty', 'mem')), may hold values from 0 to 1
- obs_cell: int32 [2097152], P(('tx', 'ty', 'mem')), may hold values from 0 to 2047
- obs_layer: int32 [2097152], P(('tx', 'ty', 'mem')), may hold values from 0 to 11
- obs_tile: int32 [2097152], P(('tx', 'ty', 'mem')), may hold values from 0 to 127, as said below
- obs_length: int32 [256], P(('tx', 'ty', 'mem')), may hold values from 4096 to 8192, as said below
- ensemble: bfloat16 [80, 6, 2, 1024, 256], P('mem', None, None, 'tx', 'ty'), may hold values from -6 to 6
Outputs:
- alpha_grad: bfloat16 [80, 2, 1024, 256], P('mem', None, 'tx', 'ty')
Inputs may be any that keep to these rules, and one draw needn't show every extreme that they name: `obs_tile`: among the 8192 entries of one device's list, padding included, at most 192 name one tile; one tile is named by exactly 192 live entries of every device's list. `obs_length`: every fourth list is full.
All inputs are finite; a program needn't handle non-finite values.
Results may differ from a plain program's by a relative error of at most 0.001.
Values sent between devices are 32-bit elements; how exact they have to be, the bound alone decides.
A program may use at most 64 MiB of HBM per device.

v0:
```python
import math

import jax
import jax.numpy as jnp
from jax import lax
from jax.sharding import PartitionSpec as P


def split_up(x, dim, length):
    before, after = (x.shape[:dim], x.shape[dim + 1 :])
    return jnp.moveaxis(x.reshape(*before, length, -1, *after), dim, 0)


def in_order(parts, dim):
    parts = jnp.moveaxis(parts, 0, dim)
    shape = parts.shape
    return parts.reshape(*shape[:dim], shape[dim] * shape[dim + 1], *shape[dim + 2 :])


def exchange_both(x, axis, axes, splits, concats):
    sizes = [lax.axis_size(a) for a in axes]
    parts = split_up(x, splits[0], sizes[0])
    parts = jnp.moveaxis(split_up(parts, splits[1] + 1, sizes[1]), 0, 1)
    inside = parts.shape[2:]
    parts = parts.reshape(-1, *inside)
    parts = lax.all_to_all(parts, axis, split_axis=0, concat_axis=0, tiled=True)
    parts = in_order(parts.reshape(*sizes, *inside), concats[0] + 1)
    return in_order(parts, concats[1])


def shifted(block, axis, distance):
    devices = range(lax.axis_size(axis))
    route = [(i - distance, i) for i in devices if i - distance in devices]
    return lax.ppermute(block, axis, route)


def copy_for_each(x, axis):
    copies = jnp.broadcast_to(x, (lax.axis_size(axis), *x.shape))
    return lax.all_to_all(copies, axis, split_axis=0, concat_axis=0, tiled=True)


def of_everyone(x, axis):
    everything = copy_for_each(x, axis)
    return jnp.sum(everything, axis=0)


def extended_2(x, sides, width):
    for axis, dim in sides:
        size, length = (lax.axis_size(axis), x.shape[dim])
        up = [(i, (i + 1) % size) for i in range(size - 1)]
        down = [(j, i) for i, j in up]
        last = lax.slice_in_dim(x, length - width, length, axis=dim)
        initial = lax.slice_in_dim(x, 0, width, axis=dim)
        before = lax.ppermute(last, axis, up)
        after = lax.ppermute(initial, axis, down)
        x = jnp.concatenate([before, x, after], axis=dim)
    return x


def smooth(padded):
    along_x = 0.25 * padded[:, :, :-2, :] + 0.5 * padded[:, :, 1:-1, :] + 0.25 * padded[:, :, 2:, :]
    return 0.25 * along_x[:, :, :, :-2] + 0.5 * along_x[:, :, :, 1:-1] + 0.25 * along_x[:, :, :, 2:]


def contract_rows(left, right):
    return lax.dot_general(
        left,
        right,
        (((0,), (0,)), ((), ())),
        precision=lax.Precision.HIGHEST,
        preferred_element_type=jnp.float32,
    )


def body(obs_value, obs_frac, obs_cell, obs_layer, obs_tile, obs_length, ensemble):
    tiles_x = lax.axis_size("tx")
    tiles_y = lax.axis_size("ty")
    tile_count = tiles_x * tiles_y
    row_count = obs_value.shape[0]
    capacity = 3 * row_count // tile_count
    slot_count = ensemble.shape[1]
    level_count = ensemble.shape[2]
    cells_x = ensemble.shape[3]
    cells_y = ensemble.shape[4]
    layer_count = slot_count * level_count
    live_rows = jnp.arange(row_count, dtype=jnp.int32) < obs_length[0]
    one_hot = (
        (obs_tile[:, None] == jnp.arange(tile_count, dtype=jnp.int32)[None, :]) & live_rows[:, None]
    ).astype(jnp.float32)
    blocks = one_hot.reshape(row_count // 128, 128, tile_count)
    lower = jnp.arange(128, dtype=jnp.int32)
    triangle = (lower[:, None] >= lower[None, :]).astype(jnp.float32)
    within = jnp.einsum("ij,bjt->bit", triangle, blocks)
    block_totals = jnp.sum(blocks, axis=1)
    offsets = jnp.cumsum(block_totals, axis=0) - block_totals
    ranking = (
        jnp.sum((within + offsets[:, None, :]) * blocks, axis=-1)
        .reshape(row_count)
        .astype(jnp.int32)
        - 1
    )
    position = obs_layer * (cells_x * cells_y) + obs_cell
    payload = jnp.stack([obs_value, obs_frac[0], obs_frac[1], position.astype(jnp.float32)], axis=1)
    send_block = math.gcd(row_count, 2048)
    slot_ids = jnp.arange(capacity, dtype=jnp.int32)

    def place_rows(step, packed):
        start = step * send_block
        hot = lax.dynamic_slice_in_dim(one_hot, start, send_block, 0)
        load = lax.dynamic_slice_in_dim(payload, start, send_block, 0)
        rank = lax.dynamic_slice_in_dim(ranking, start, send_block, 0)
        slots = (rank[:, None] == slot_ids[None, :]).astype(jnp.float32)
        left = (load[:, :, None] * hot[:, None, :]).reshape(send_block, 4 * tile_count)
        return packed + contract_rows(left, slots)

    packed = lax.fori_loop(
        0, row_count // send_block, place_rows, jnp.zeros((4 * tile_count, capacity), jnp.float32)
    )
    packed = packed.reshape(4, tile_count, capacity)
    send_floats = packed[:3]
    send_index = packed[3:4].astype(jnp.int32)
    sectioned = (
        exchange_both(
            send_floats.reshape(3, tiles_x, tiles_y, capacity),
            ("tx", "ty"),
            ("tx", "ty"),
            (1, 2),
            (1, 2),
        ),
        exchange_both(
            send_index.reshape(1, tiles_x, tiles_y, capacity),
            ("tx", "ty"),
            ("tx", "ty"),
            (1, 2),
            (1, 2),
        ),
    )
    got_floats = sectioned[0].reshape(3, tile_count, capacity)
    got_index = sectioned[1].reshape(1, tile_count, capacity)
    got_count = tile_count * capacity
    values = got_floats[0].reshape(-1)
    frac_x = got_floats[1].reshape(-1)
    frac_y = got_floats[2].reshape(-1)
    spot = got_index[0].reshape(-1)
    layer = spot // (cells_x * cells_y)
    column = spot % (cells_x * cells_y)
    column_x = column // cells_y
    column_y = column % cells_y
    recv_block = math.gcd(got_count, 2048)
    layer_ids = jnp.arange(layer_count, dtype=jnp.int32)
    xs_ids = jnp.arange(cells_x + 1, dtype=jnp.int32)
    ys_ids = jnp.arange(cells_y, dtype=jnp.int32)

    def spread_rows(step, carry):
        main, rim = carry
        start = step * recv_block
        val = lax.dynamic_slice_in_dim(values, start, recv_block, 0)
        wfx = lax.dynamic_slice_in_dim(frac_x, start, recv_block, 0)
        wfy = lax.dynamic_slice_in_dim(frac_y, start, recv_block, 0)
        lay = lax.dynamic_slice_in_dim(layer, start, recv_block, 0)
        colx = lax.dynamic_slice_in_dim(column_x, start, recv_block, 0)
        coly = lax.dynamic_slice_in_dim(column_y, start, recv_block, 0)
        layer_hot = jnp.where(lay[:, None] == layer_ids[None, :], val[:, None], jnp.float32(0.0))
        weight_x = jnp.where(colx[:, None] == xs_ids[None, :], 1.0 - wfx[:, None], jnp.float32(0.0))
        weight_x = weight_x + jnp.where(
            colx[:, None] + 1 == xs_ids[None, :], wfx[:, None], jnp.float32(0.0)
        )
        weight_y = jnp.where(coly[:, None] == ys_ids[None, :], 1.0 - wfy[:, None], jnp.float32(0.0))
        weight_y = weight_y + jnp.where(
            coly[:, None] + 1 == ys_ids[None, :], wfy[:, None], jnp.float32(0.0)
        )
        rim_weight = jnp.where(coly + 1 == cells_y, wfy, jnp.float32(0.0))
        left = (layer_hot[:, :, None] * weight_x[:, None, :]).reshape(
            recv_block, layer_count * (cells_x + 1)
        )
        main = main + contract_rows(left, weight_y)
        rim = rim + contract_rows(left, rim_weight)
        return (main, rim)

    start_main = jnp.zeros((layer_count * (cells_x + 1), cells_y), jnp.float32)
    start_rim = jnp.zeros((layer_count * (cells_x + 1),), jnp.float32)
    main, rim = lax.fori_loop(0, got_count // recv_block, spread_rows, (start_main, start_rim))
    extended = main.reshape(layer_count, cells_x + 1, cells_y)
    interior = extended[:, :cells_x, :]
    east_rim = extended[:, cells_x, :]
    north_rim = rim.reshape(layer_count, cells_x + 1)
    from_south = shifted(north_rim, "ty", 1)
    interior = interior.at[:, :, 0].add(from_south[:, :cells_x])
    east_rim = east_rim.at[:, 0].add(from_south[:, cells_x])
    from_west = shifted(east_rim, "tx", 1)
    interior = interior.at[:, 0, :].add(from_west)
    grad = of_everyone(interior, "mem")
    grad_slots = grad.reshape(slot_count, level_count, cells_x, cells_y)
    contrib = jnp.sum(ensemble * grad_slots[None], axis=1)
    padded = extended_2(contrib, (("tx", 2), ("ty", 3)), 1)
    return smooth(padded).astype(jnp.bfloat16)


def solution(mesh):
    placed = (
        P(("tx", "ty", "mem")),
        P(None, ("tx", "ty", "mem")),
        P(("tx", "ty", "mem")),
        P(("tx", "ty", "mem")),
        P(("tx", "ty", "mem")),
        P(("tx", "ty", "mem")),
        P("mem", None, None, "tx", "ty"),
    )
    return jax.shard_map(
        body, mesh=mesh, in_specs=placed, out_specs=P("mem", None, "tx", "ty"), check_vma=False
    )
```

profile of v0, /device:TPU:28, one launch (start us, length us, event | category | flops | bytes accessed | tf_op | source)
XLA Modules:
  0.0 258.9 jit_solution(15534617041825692092)
XLA Ops:
  0.7 1.9 convert_reduce_fusion
  2.7 3.2 %fusion.25 = f32[64,128]{1,0:T(8,128)S(1)} fusion(f32[64,128]{1,0:T(8,128)S(1)} %sub.39, s32[64,128]{1,0:T(8,128)} %bitcast.99, pred[64,128]{1,0:T(8,128)(4,1)S(1)} %add_compare_fusion), kind=kOutput, calls=%fused_computation.38 | convolution fusion | flops 275783680 | bytes 106496 | tf_op jit(solution)/shard_map/ij,bjt->bit/dot_general | solution.py:93
  6.0 4.9 %fusion.27 = f32[8192,128]{1,0:T(8,128)} fusion(s32[8192]{0:T(1024)S(1)} %copy-done.2, pred[8192]{0:T(1024)(128)(4,1)S(1)} %iota_compare_fusion.14), kind=kLoop, calls=%fused_computation.43 | loop fusion | flops 3145728 | bytes 4235264 | tf_op jit(solution)/shard_map/convert_element_type | solution.py:89
  11.1 61.6 %while.34 = (s32[]{:T(128)}, f32[512,192]{0,1:T(8,128)S(1)}, f32[8192,4]{0,1:T(4,128)S(1)}, f32[8192,128]{1,0:T(8,128)}, s32[8192]{0:T(1024)S(1)}, /*index=5*/s32[]{:T(128)}, s32[]{:T(128)}, s32[]{:T(128)}, s32[]{:T(128)}) while((s32[]{:T(128)}, f32[512,192]{0,1:T(8,128)S(1)}, f32[8192,4]{0,1:T(4,128)S(1)}, f32[8192,128]{1,0:T(8,128)}, ...), condition=%wide.region_4.5_spmd.clone, body=%wide.region_3.4_spmd.clone.sunk | while | flops 2417557504 | bytes 12509345 | solution.py:116
  12.8 8.7 %broadcast_multiply_fusion.4 = f32[2048,4,128]{2,1,0:T(4,128)} fusion(f32[2048,128]{1,0:T(8,128)S(1)} %constant_dynamic-slice_fusion.4, f32[2048,4]{1,0:T(8,128)S(1)} %copy.138), kind=kLoop, calls=%fused_computation.8.clone.1 | loop fusion | flops 1048576 | bytes 5275648 | tf_op jit(solution)/shard_map/while/body/eval_jaxpr/mul | solution.py:113
  21.5 5.0 %fusion.63 = f32[512,192]{0,1:T(8,128)S(1)} fusion(f32[256,8,4,128]{3,2,1,0:T(4,128)} %bitcast.90, s32[2048]{0:T(1024)S(1)} %dynamic_slice.94, f32[512,192]{0,1:T(8,128)S(1)} %get-tuple-element.605, pred[]{:T(512)S(6)} %compare.33), kind=kOutput, calls=%fused_computation.9.clone.1 | convolution fusion | flops 2416508928 | bytes 4988929 | tf_op jit(solution)/shard_map/while/body/eval_jaxpr/dot_general | solution.py:66
  28.2 8.7 %broadcast_multiply_fusion.4 = f32[2048,4,128]{2,1,0:T(4,128)} fusion(f32[2048,128]{1,0:T(8,128)S(1)} %constant_dynamic-slice_fusion.4, f32[2048,4]{1,0:T(8,128)S(1)} %copy.138), kind=kLoop, calls=%fused_computation.8.clone.1 | loop fusion | flops 1048576 | bytes 5275648 | tf_op jit(solution)/shard_map/while/body/eval_jaxpr/mul | solution.py:113
  36.9 5.0 %fusion.63 = f32[512,192]{0,1:T(8,128)S(1)} fusion(f32[256,8,4,128]{3,2,1,0:T(4,128)} %bitcast.90, s32[2048]{0:T(1024)S(1)} %dynamic_slice.94, f32[512,192]{0,1:T(8,128)S(1)} %get-tuple-element.605, pred[]{:T(512)S(6)} %compare.33), kind=kOutput, calls=%fused_computation.9.clone.1 | convolution fusion | flops 2416508928 | bytes 4988929 | tf_op jit(solution)/shard_map/while/body/eval_jaxpr/dot_general | solution.py:66
  43.6 8.7 %broadcast_multiply_fusion.4 = f32[2048,4,128]{2,1,0:T(4,128)} fusion(f32[2048,128]{1,0:T(8,128)S(1)} %constant_dynamic-slice_fusion.4, f32[2048,4]{1,0:T(8,128)S(1)} %copy.138), kind=kLoop, calls=%fused_computation.8.clone.1 | loop fusion | flops 1048576 | bytes 5275648 | tf_op jit(solution)/shard_map/while/body/eval_jaxpr/mul | solution.py:113
  52.3 5.0 %fusion.63 = f32[512,192]{0,1:T(8,128)S(1)} fusion(f32[256,8,4,128]{3,2,1,0:T(4,128)} %bitcast.90, s32[2048]{0:T(1024)S(1)} %dynamic_slice.94, f32[512,192]{0,1:T(8,128)S(1)} %get-tuple-element.605, pred[]{:T(512)S(6)} %compare.33), kind=kOutput, calls=%fused_computation.9.clone.1 | convolution fusion | flops 2416508928 | bytes 4988929 | tf_op jit(solution)/shard_map/while/body/eval_jaxpr/dot_general | solution.py:66
  59.0 8.7 %broadcast_multiply_fusion.4 = f32[2048,4,128]{2,1,0:T(4,128)} fusion(f32[2048,128]{1,0:T(8,128)S(1)} %constant_dynamic-slice_fusion.4, f32[2048,4]{1,0:T(8,128)S(1)} %copy.138), kind=kLoop, calls=%fused_computation.8.clone.1 | loop fusion | flops 1048576 | bytes 5275648 | tf_op jit(solution)/shard_map/while/body/eval_jaxpr/mul | solution.py:113
  67.7 5.0 %fusion.63 = f32[512,192]{0,1:T(8,128)S(1)} fusion(f32[256,8,4,128]{3,2,1,0:T(4,128)} %bitcast.90, s32[2048]{0:T(1024)S(1)} %dynamic_slice.94, f32[512,192]{0,1:T(8,128)S(1)} %get-tuple-element.605, pred[]{:T(512)S(6)} %compare.33), kind=kOutput, calls=%fused_computation.9.clone.1 | convolution fusion | flops 2416508928 | bytes 4988929 | tf_op jit(solution)/shard_map/while/body/eval_jaxpr/dot_general | solution.py:66
  73.5 15.1 %all-to-all-start = ((s32[128,1,1,1,192]{4,3,2,1,0:T(1,128)}), s32[128,1,1,1,192]{4,3,2,1,0:T(1,128)S(1)}, u32[]{:S(2)}, u32[]{:S(2)}) async-start(s32[128,1,1,1,192]{4,3,2,1,0:T(1,128)} %copy.91), calls=%async_computation | async-start | bytes 262144 | tf_op jit(solution)/shard_map/all_to_all | solution.py:26
  90.2 7.2 %all-to-all-done = s32[128,1,1,1,192]{4,3,2,1,0:T(1,128)S(1)} async-done(((s32[128,1,1,1,192]{4,3,2,1,0:T(1,128)}), s32[128,1,1,1,192]{4,3,2,1,0:T(1,128)S(1)}, u32[]{:S(2)}, u32[]{:S(2)}) %all-to-all-start) | async-done | bytes 98336 | tf_op jit(solution)/shard_map/all_to_all | solution.py:26
  97.4 9.7 %all-to-all-start.1 = ((f32[128,3,1,1,192]{4,3,1,2,0:T(1,128)}), f32[128,3,1,1,192]{4,3,1,2,0:T(1,128)S(1)}, u32[]{:S(2)}, u32[]{:S(2)}) async-start(f32[128,3,1,1,192]{4,3,1,2,0:T(1,128)} %bitcast.17), calls=%async_computation.1 | async-start | bytes 786432 | tf_op jit(solution)/shard_map/all_to_all | solution.py:26
  107.5 12.8 %all-to-all-done.1 = f32[128,3,1,1,192]{4,3,1,2,0:T(1,128)S(1)} async-done(((f32[128,3,1,1,192]{4,3,1,2,0:T(1,128)}), f32[128,3,1,1,192]{4,3,1,2,0:T(1,128)S(1)}, u32[]{:S(2)}, u32[]{:S(2)}) %all-to-all-start.1) | async-done | bytes 294944 | tf_op jit(solution)/shard_map/all_to_all | solution.py:26
  121.2 87.0 %while.35 = (s32[]{:T(128)}, f32[204,128]{1,0:T(8,128)S(1)}, f32[204]{0:T(256)S(1)}, s32[24576]{0:T(1024)S(1)}, f32[24576]{0:T(1024)S(1)}, /*index=5*/s32[24576]...) while((s32[]{:T(128)}, f32[204,128]{1,0:T(8,128)S(1)}, ...), condition=%wide.region_6.7_spmd.clone.clone, body=%wide.region_5.6_spmd.clone.clone.sunk | while | flops 648760704 | bytes 15973794 | solution.py:182
  121.7 1.4 mul.212
  123.1 3.9 %convolution_add_fusion.2 = f32[204,128]{1,0:T(8,128)S(1)} fusion(f32[2048,204]{0,1:T(8,128)} %mul.212, f32[2048]{0:T(1024)S(1)} %get-tuple-element.592, s32[2048]{0:T(1024)S(1)} %broadcast_add_fusion.5, f32[2048]{0:T(1024)S(1)} %broadcast_subtract_fusion.3, s32[2048]{0:T(1024)S(1)} %get-tuple-element.593, f32[204,128]{1,0:T(8,128)S(1)} %get-tuple-element.636, ...), kind=kOutput, calls=%fused_computation.16.clone.1 | convolution fusion | flops 643091456 | bytes 1912833 | tf_op jit(solution)/shard_map/while/body/eval_jaxpr/dot_general | solution.py:66
  128.9 1.4 mul.212
  130.4 3.9 %convolution_add_fusion.2 = f32[204,128]{1,0:T(8,128)S(1)} fusion(f32[2048,204]{0,1:T(8,128)} %mul.212, f32[2048]{0:T(1024)S(1)} %get-tuple-element.592, s32[2048]{0:T(1024)S(1)} %broadcast_add_fusion.5, f32[2048]{0:T(1024)S(1)} %broadcast_subtract_fusion.3, s32[2048]{0:T(1024)S(1)} %get-tuple-element.593, f32[204,128]{1,0:T(8,128)S(1)} %get-tuple-element.636, ...), kind=kOutput, calls=%fused_computation.16.clone.1 | convolution fusion | flops 643091456 | bytes 1912833 | tf_op jit(solution)/shard_map/while/body/eval_jaxpr/dot_general | solution.py:66
  136.2 1.4 mul.212
  137.6 3.9 %convolution_add_fusion.2 = f32[204,128]{1,0:T(8,128)S(1)} fusion(f32[2048,204]{0,1:T(8,128)} %mul.212, f32[2048]{0:T(1024)S(1)} %get-tuple-element.592, s32[2048]{0:T(1024)S(1)} %broadcast_add_fusion.5, f32[2048]{0:T(1024)S(1)} %broadcast_subtract_fusion.3, s32[2048]{0:T(1024)S(1)} %get-tuple-element.593, f32[204,128]{1,0:T(8,128)S(1)} %get-tuple-element.636, ...), kind=kOutput, calls=%fused_computation.16.clone.1 | convolution fusion | flops 643091456 | bytes 1912833 | tf_op jit(solution)/shard_map/while/body/eval_jaxpr/dot_general | solution.py:66
  143.4 1.4 mul.212
  144.9 3.9 %convolution_add_fusion.2 = f32[204,128]{1,0:T(8,128)S(1)} fusion(f32[2048,204]{0,1:T(8,128)} %mul.212, f32[2048]{0:T(1024)S(1)} %get-tuple-element.592, s32[2048]{0:T(1024)S(1)} %broadcast_add_fusion.5, f32[2048]{0:T(1024)S(1)} %broadcast_subtract_fusion.3, s32[2048]{0:T(1024)S(1)} %get-tuple-element.593, f32[204,128]{1,0:T(8,128)S(1)} %get-tuple-element.636, ...), kind=kOutput, calls=%fused_computation.16.clone.1 | convolution fusion | flops 643091456 | bytes 1912833 | tf_op jit(solution)/shard_map/while/body/eval_jaxpr/dot_general | solution.py:66
  150.7 1.4 mul.212
  152.1 3.9 %convolution_add_fusion.2 = f32[204,128]{1,0:T(8,128)S(1)} fusion(f32[2048,204]{0,1:T(8,128)} %mul.212, f32[2048]{0:T(1024)S(1)} %get-tuple-element.592, s32[2048]{0:T(1024)S(1)} %broadcast_add_fusion.5, f32[2048]{0:T(1024)S(1)} %broadcast_subtract_fusion.3, s32[2048]{0:T(1024)S(1)} %get-tuple-element.593, f32[204,128]{1,0:T(8,128)S(1)} %get-tuple-element.636, ...), kind=kOutput, calls=%fused_computation.16.clone.1 | convolution fusion | flops 643091456 | bytes 1912833 | tf_op jit(solution)/shard_map/while/body/eval_jaxpr/dot_general | solution.py:66
  157.9 1.4 mul.212
  159.4 3.9 %convolution_add_fusion.2 = f32[204,128]{1,0:T(8,128)S(1)} fusion(f32[2048,204]{0,1:T(8,128)} %mul.212, f32[2048]{0:T(1024)S(1)} %get-tuple-element.592, s32[2048]{0:T(1024)S(1)} %broadcast_add_fusion.5, f32[2048]{0:T(1024)S(1)} %broadcast_subtract_fusion.3, s32[2048]{0:T(1024)S(1)} %get-tuple-element.593, f32[204,128]{1,0:T(8,128)S(1)} %get-tuple-element.636, ...), kind=kOutput, calls=%fused_computation.16.clone.1 | convolution fusion | flops 643091456 | bytes 1912833 | tf_op jit(solution)/shard_map/while/body/eval_jaxpr/dot_general | solution.py:66
  165.2 1.4 mul.212
  166.6 3.9 %convolution_add_fusion.2 = f32[204,128]{1,0:T(8,128)S(1)} fusion(f32[2048,204]{0,1:T(8,128)} %mul.212, f32[2048]{0:T(1024)S(1)} %get-tuple-element.592, s32[2048]{0:T(1024)S(1)} %broadcast_add_fusion.5, f32[2048]{0:T(1024)S(1)} %broadcast_subtract_fusion.3, s32[2048]{0:T(1024)S(1)} %get-tuple-element.593, f32[204,128]{1,0:T(8,128)S(1)} %get-tuple-element.636, ...), kind=kOutput, calls=%fused_computation.16.clone.1 | convolution fusion | flops 643091456 | bytes 1912833 | tf_op jit(solution)/shard_map/while/body/eval_jaxpr/dot_general | solution.py:66
  172.4 1.4 mul.212
  173.9 3.9 %convolution_add_fusion.2 = f32[204,128]{1,0:T(8,128)S(1)} fusion(f32[2048,204]{0,1:T(8,128)} %mul.212, f32[2048]{0:T(1024)S(1)} %get-tuple-element.592, s32[2048]{0:T(1024)S(1)} %broadcast_add_fusion.5, f32[2048]{0:T(1024)S(1)} %broadcast_subtract_fusion.3, s32[2048]{0:T(1024)S(1)} %get-tuple-element.593, f32[204,128]{1,0:T(8,128)S(1)} %get-tuple-element.636, ...), kind=kOutput, calls=%fused_computation.16.clone.1 | convolution fusion | flops 643091456 | bytes 1912833 | tf_op jit(solution)/shard_map/while/body/eval_jaxpr/dot_general | solution.py:66
  179.7 1.4 mul.212
  181.1 3.9 %convolution_add_fusion.2 = f32[204,128]{1,0:T(8,128)S(1)} fusion(f32[2048,204]{0,1:T(8,128)} %mul.212, f32[2048]{0:T(1024)S(1)} %get-tuple-element.592, s32[2048]{0:T(1024)S(1)} %broadcast_add_fusion.5, f32[2048]{0:T(1024)S(1)} %broadcast_subtract_fusion.3, s32[2048]{0:T(1024)S(1)} %get-tuple-element.593, f32[204,128]{1,0:T(8,128)S(1)} %get-tuple-element.636, ...), kind=kOutput, calls=%fused_computation.16.clone.1 | convolution fusion | flops 643091456 | bytes 1912833 | tf_op jit(solution)/shard_map/while/body/eval_jaxpr/dot_general | solution.py:66
  186.9 1.4 mul.212
  188.4 3.9 %convolution_add_fusion.2 = f32[204,128]{1,0:T(8,128)S(1)} fusion(f32[2048,204]{0,1:T(8,128)} %mul.212, f32[2048]{0:T(1024)S(1)} %get-tuple-element.592, s32[2048]{0:T(1024)S(1)} %broadcast_add_fusion.5, f32[2048]{0:T(1024)S(1)} %broadcast_subtract_fusion.3, s32[2048]{0:T(1024)S(1)} %get-tuple-element.593, f32[204,128]{1,0:T(8,128)S(1)} %get-tuple-element.636, ...), kind=kOutput, calls=%fused_computation.16.clone.1 | convolution fusion | flops 643091456 | bytes 1912833 | tf_op jit(solution)/shard_map/while/body/eval_jaxpr/dot_general | solution.py:66
  195.6 3.9 %convolution_add_fusion.2 = f32[204,128]{1,0:T(8,128)S(1)} fusion(f32[2048,204]{0,1:T(8,128)} %mul.212, f32[2048]{0:T(1024)S(1)} %get-tuple-element.592, s32[2048]{0:T(1024)S(1)} %broadcast_add_fusion.5, f32[2048]{0:T(1024)S(1)} %broadcast_subtract_fusion.3, s32[2048]{0:T(1024)S(1)} %get-tuple-element.593, f32[204,128]{1,0:T(8,128)S(1)} %get-tuple-element.636, ...), kind=kOutput, calls=%fused_computation.16.clone.1 | convolution fusion | flops 643091456 | bytes 1912833 | tf_op jit(solution)/shard_map/while/body/eval_jaxpr/dot_general | solution.py:66
  201.4 1.4 mul.212
  202.9 3.9 %convolution_add_fusion.2 = f32[204,128]{1,0:T(8,128)S(1)} fusion(f32[2048,204]{0,1:T(8,128)} %mul.212, f32[2048]{0:T(1024)S(1)} %get-tuple-element.592, s32[2048]{0:T(1024)S(1)} %broadcast_add_fusion.5, f32[2048]{0:T(1024)S(1)} %broadcast_subtract_fusion.3, s32[2048]{0:T(1024)S(1)} %get-tuple-element.593, f32[204,128]{1,0:T(8,128)S(1)} %get-tuple-element.636, ...), kind=kOutput, calls=%fused_computation.16.clone.1 | convolution fusion | flops 643091456 | bytes 1912833 | tf_op jit(solution)/shard_map/while/body/eval_jaxpr/dot_general | solution.py:66
  208.3 3.0 %collective-permute-start = (f32[12,17]{1,0:T(8,128)S(1)}, f32[12,17]{1,0:T(8,128)S(1)}, u32[]{:S(2)}, u32[]{:S(2)}) collective-permute-start(f32[12,17]{1,0:T(8,128)S(1)} %reshape.322), channel_id=1, source_target_pairs={{0,2},{1,3},{4,6},{5,7},{8,10},{9,11},{12,14},{13,15},{16,18},{17,... | collective-permute-start | bytes 2456 | tf_op jit(solution)/shard_map/ppermute | solution.py:34
  213.5 6.1 %collective-permute-start.1 = (f32[12,128]{1,0:T(8,128)S(1)}, f32[12,128]{1,0:T(8,128)S(1)}, u32[]{:S(2)}, u32[]{:S(2)}) collective-permute-start(f32[12,128]{1,0:T(8,128)S(1)} %scatter-add.11), channel_id=1, source_target_pairs={{0,4},{4,8},{8,12},{12,16},{16,20},{20,24},{24,28},{28,32},{32,36}... | collective-permute-start | bytes 18440 | tf_op jit(solution)/shard_map/ppermute | solution.py:34
  221.0 3.9 %all_to_all.15 = f32[2,12,16,128]{3,2,1,0:T(8,128)S(1)} all-to-all(f32[2,12,16,128]{3,2,1,0:T(8,128)S(1)} %broadcast_in_dim.170), channel_id=1, replica_groups=mesh['tx'=64,'ty'=2,'mem'=2] {'mem'}, dimensions={0} | all-to-all | bytes 393216 | tf_op jit(solution)/shard_map/all_to_all | solution.py:39
  225.4 8.7 %collective-permute-start.2 = (f32[40,2,1,128]{3,0,2,1:T(8,128)S(1)}, f32[40,2,1,128]{3,0,2,1:T(8,128)S(1)}, u32[]{:S(2)}, u32[]{:S(2)}) collective-permute-start(f32[40,2,1,128]{3,0,2,1:T(8,128)S(1)} %copy.105), channel_id=1, source_target_pairs={{0,4},{4,8},{8,12},{12,16},{16,20},{20,24},{24,28},{28,32},{32,36}... | collective-permute-start | bytes 122888 | tf_op jit(solution)/shard_map/ppermute | solution.py:54
  234.2 1.9 collective-permute-start.3
  236.2 8.5 %collective-permute-done.3 = f32[40,2,1,128]{3,0,2,1:T(8,128)S(1)} collective-permute-done((f32[40,2,1,128]{3,0,2,1:T(8,128)S(1)}, f32[40,2,1,128]{3,0,2,1:T(8,128)S(1)}, u32[]{:S(2)}, u32[]{:S(2)}) %collective-permute-start.3) | collective-permute-done | bytes 40992 | tf_op jit(solution)/shard_map/ppermute | solution.py:55
  245.7 4.7 %collective-permute-start.4 = (f32[40,2,18,1]{0,2,3,1:T(8,128)S(1)}, f32[40,2,18,1]{0,2,3,1:T(8,128)S(1)}, u32[]{:S(2)}, u32[]{:S(2)}) collective-permute-start(f32[40,2,18,1]{0,2,3,1:T(8,128)S(1)} %copy.109), channel_id=1, source_target_pairs={{0,2},{1,3},{4,6},{5,7},{8,10},{9,11},{12,14},{13,15},{16,18},{17,... | collective-permute-start | bytes 17288 | tf_op jit(solution)/shard_map/ppermute | solution.py:54
  252.7 3.8 %collective-permute-done.5 = f32[40,2,18,1]{0,2,3,1:T(8,128)S(1)} collective-permute-done((f32[40,2,18,1]{0,2,3,1:T(8,128)S(1)}, f32[40,2,18,1]{0,2,3,1:T(8,128)S(1)}, u32[]{:S(2)}, u32[]{:S(2)}) %collective-permute-start.5) | collective-permute-done | bytes 5792 | tf_op jit(solution)/shard_map/ppermute | solution.py:55
  (254 shorter events, 43.5 us)
Async XLA Ops:
  2.7 3.2 %copy-start.3 = (f32[2,8192]{1,0:T(2,128)S(1)}, f32[2,8192]{1,0:T(2,128)}, u32[]{:S(2)}) copy-start(f32[2,8192]{1,0:T(2,128)} %param.18) | copy-start | bytes 196612
  2.7 3.3 %copy-start.2 = (s32[8192]{0:T(1024)S(1)}, s32[8192]{0:T(1024)}, u32[]{:S(2)}) copy-start(s32[8192]{0:T(1024)} %param.21) | copy-start | bytes 98308
  5.9 5.1 %copy-start.4 = (s32[8192]{0:T(1024)S(1)}, s32[8192]{0:T(1024)}, u32[]{:S(2)}) copy-start(s32[8192]{0:T(1024)} %param.19) | copy-start | bytes 98308
  5.9 5.1 %copy-start.5 = (s32[8192]{0:T(1024)S(1)}, s32[8192]{0:T(1024)}, u32[]{:S(2)}) copy-start(s32[8192]{0:T(1024)} %param.20) | copy-start | bytes 98308
  5.9 5.1 %copy-start.6 = (f32[8192]{0:T(1024)S(1)}, f32[8192]{0:T(1024)}, u32[]{:S(2)}) copy-start(f32[8192]{0:T(1024)} %param.17) | copy-start | bytes 98308
  73.5 23.9 %all-to-all-start = ((s32[128,1,1,1,192]{4,3,2,1,0:T(1,128)}), s32[128,1,1,1,192]{4,3,2,1,0:T(1,128)S(1)}, u32[]{:S(2)}, u32[]{:S(2)}) async-start(s32[128,1,1,1,192]{4,3,2,1,0:T(1,128)} %copy.91), calls=%async_computation | async-start | bytes 262144 | tf_op jit(solution)/shard_map/all_to_all | solution.py:26
  97.4 23.0 %all-to-all-start.1 = ((f32[128,3,1,1,192]{4,3,1,2,0:T(1,128)}), f32[128,3,1,1,192]{4,3,1,2,0:T(1,128)S(1)}, u32[]{:S(2)}, u32[]{:S(2)}) async-start(f32[128,3,1,1,192]{4,3,1,2,0:T(1,128)} %bitcast.17), calls=%async_computation.1 | async-start | bytes 786432 | tf_op jit(solution)/shard_map/all_to_all | solution.py:26
  123.1 3.9 %copy-start = (f32[2048,204]{0,1:T(8,128)S(1)}, f32[2048,204]{0,1:T(8,128)}, u32[]{:S(2)}) copy-start(f32[2048,204]{0,1:T(8,128)} %mul.212) | copy-start | bytes 5013508 | tf_op jit(solution)/shard_map/while
  130.3 3.9 %copy-start = (f32[2048,204]{0,1:T(8,128)S(1)}, f32[2048,204]{0,1:T(8,128)}, u32[]{:S(2)}) copy-start(f32[2048,204]{0,1:T(8,128)} %mul.212) | copy-start | bytes 5013508 | tf_op jit(solution)/shard_map/while
  137.6 3.9 %copy-start = (f32[2048,204]{0,1:T(8,128)S(1)}, f32[2048,204]{0,1:T(8,128)}, u32[]{:S(2)}) copy-start(f32[2048,204]{0,1:T(8,128)} %mul.212) | copy-start | bytes 5013508 | tf_op jit(solution)/shard_map/while
  144.8 3.9 %copy-start = (f32[2048,204]{0,1:T(8,128)S(1)}, f32[2048,204]{0,1:T(8,128)}, u32[]{:S(2)}) copy-start(f32[2048,204]{0,1:T(8,128)} %mul.212) | copy-start | bytes 5013508 | tf_op jit(solution)/shard_map/while
  152.1 3.9 %copy-start = (f32[2048,204]{0,1:T(8,128)S(1)}, f32[2048,204]{0,1:T(8,128)}, u32[]{:S(2)}) copy-start(f32[2048,204]{0,1:T(8,128)} %mul.212) | copy-start | bytes 5013508 | tf_op jit(solution)/shard_map/while
  159.4 3.9 %copy-start = (f32[2048,204]{0,1:T(8,128)S(1)}, f32[2048,204]{0,1:T(8,128)}, u32[]{:S(2)}) copy-start(f32[2048,204]{0,1:T(8,128)} %mul.212) | copy-start | bytes 5013508 | tf_op jit(solution)/shard_map/while
  166.6 3.9 %copy-start = (f32[2048,204]{0,1:T(8,128)S(1)}, f32[2048,204]{0,1:T(8,128)}, u32[]{:S(2)}) copy-start(f32[2048,204]{0,1:T(8,128)} %mul.212) | copy-start | bytes 5013508 | tf_op jit(solution)/shard_map/while
  173.9 3.9 %copy-start = (f32[2048,204]{0,1:T(8,128)S(1)}, f32[2048,204]{0,1:T(8,128)}, u32[]{:S(2)}) copy-start(f32[2048,204]{0,1:T(8,128)} %mul.212) | copy-start | bytes 5013508 | tf_op jit(solution)/shard_map/while
  181.1 3.9 %copy-start = (f32[2048,204]{0,1:T(8,128)S(1)}, f32[2048,204]{0,1:T(8,128)}, u32[]{:S(2)}) copy-start(f32[2048,204]{0,1:T(8,128)} %mul.212) | copy-start | bytes 5013508 | tf_op jit(solution)/shard_map/while
  188.4 3.9 %copy-start = (f32[2048,204]{0,1:T(8,128)S(1)}, f32[2048,204]{0,1:T(8,128)}, u32[]{:S(2)}) copy-start(f32[2048,204]{0,1:T(8,128)} %mul.212) | copy-start | bytes 5013508 | tf_op jit(solution)/shard_map/while
  195.6 3.9 %copy-start = (f32[2048,204]{0,1:T(8,128)S(1)}, f32[2048,204]{0,1:T(8,128)}, u32[]{:S(2)}) copy-start(f32[2048,204]{0,1:T(8,128)} %mul.212) | copy-start | bytes 5013508 | tf_op jit(solution)/shard_map/while
  202.9 3.9 %copy-start = (f32[2048,204]{0,1:T(8,128)S(1)}, f32[2048,204]{0,1:T(8,128)}, u32[]{:S(2)}) copy-start(f32[2048,204]{0,1:T(8,128)} %mul.212) | copy-start | bytes 5013508 | tf_op jit(solution)/shard_map/while
  208.2 16.7 %copy-start.1 = (bf16[40,6,2,16,128]{4,3,2,1,0:T(8,128)(2,1)S(1)}, bf16[40,6,2,16,128]{4,3,2,1,0:T(8,128)(2,1)}, u32[]{:S(2)}) copy-start(bf16[40,6,2,16,128]{4,3,2,1,0:T(8,128)(2,1)} %param.23) | copy-start | bytes 5898244
  208.3 4.4 %collective-permute-start = (f32[12,17]{1,0:T(8,128)S(1)}, f32[12,17]{1,0:T(8,128)S(1)}, u32[]{:S(2)}, u32[]{:S(2)}) collective-permute-start(f32[12,17]{1,0:T(8,128)S(1)} %reshape.322), channel_id=1, source_target_pairs={{0,2},{1,3},{4,6},{5,7},{8,10},{9,11},{12,14},{13,15},{16,18},{17,... | collective-permute-start | bytes 2456 | tf_op jit(solution)/shard_map/ppermute | solution.py:34
  213.5 7.5 %collective-permute-start.1 = (f32[12,128]{1,0:T(8,128)S(1)}, f32[12,128]{1,0:T(8,128)S(1)}, u32[]{:S(2)}, u32[]{:S(2)}) collective-permute-start(f32[12,128]{1,0:T(8,128)S(1)} %scatter-add.11), channel_id=1, source_target_pairs={{0,4},{4,8},{8,12},{12,16},{16,20},{20,24},{24,28},{28,32},{32,36}... | collective-permute-start | bytes 18440 | tf_op jit(solution)/shard_map/ppermute | solution.py:34
  225.4 10.7 %collective-permute-start.2 = (f32[40,2,1,128]{3,0,2,1:T(8,128)S(1)}, f32[40,2,1,128]{3,0,2,1:T(8,128)S(1)}, u32[]{:S(2)}, u32[]{:S(2)}) collective-permute-start(f32[40,2,1,128]{3,0,2,1:T(8,128)S(1)} %copy.105), channel_id=1, source_target_pairs={{0,4},{4,8},{8,12},{12,16},{16,20},{20,24},{24,28},{28,32},{32,36}... | collective-permute-start | bytes 122888 | tf_op jit(solution)/shard_map/ppermute | solution.py:54
  234.2 10.5 %collective-permute-start.3 = (f32[40,2,1,128]{3,0,2,1:T(8,128)S(1)}, f32[40,2,1,128]{3,0,2,1:T(8,128)S(1)}, u32[]{:S(2)}, u32[]{:S(2)}) collective-permute-start(f32[40,2,1,128]{3,0,2,1:T(8,128)S(1)} %copy.106), channel_id=1, source_target_pairs={{4,0},{8,4},{12,8},{16,12},{20,16},{24,20},{28,24},{32,28},{36,32}... | collective-permute-start | bytes 122888 | tf_op jit(solution)/shard_map/ppermute | solution.py:55
  245.7 6.7 %collective-permute-start.4 = (f32[40,2,18,1]{0,2,3,1:T(8,128)S(1)}, f32[40,2,18,1]{0,2,3,1:T(8,128)S(1)}, u32[]{:S(2)}, u32[]{:S(2)}) collective-permute-start(f32[40,2,18,1]{0,2,3,1:T(8,128)S(1)} %copy.109), channel_id=1, source_target_pairs={{0,2},{1,3},{4,6},{5,7},{8,10},{9,11},{12,14},{13,15},{16,18},{17,... | collective-permute-start | bytes 17288 | tf_op jit(solution)/shard_map/ppermute | solution.py:54
  250.8 5.7 %collective-permute-start.5 = (f32[40,2,18,1]{0,2,3,1:T(8,128)S(1)}, f32[40,2,18,1]{0,2,3,1:T(8,128)S(1)}, u32[]{:S(2)}, u32[]{:S(2)}) collective-permute-start(f32[40,2,18,1]{0,2,3,1:T(8,128)S(1)} %copy.110), channel_id=1, source_target_pairs={{2,0},{3,1},{6,4},{7,5},{10,8},{11,9},{14,12},{15,13},{18,16},{19,... | collective-permute-start | bytes 17288 | tf_op jit(solution)/shard_map/ppermute | solution.py:55
where the time goes:
time: 260 us; the launch traced here: 259 us
  matrix products  87 us (33%)
  starting transfers between devices  50.5 us (19%)
  other arithmetic  49.7 us (19%)
  waiting for transfers between devices  34 us (13%)
  local copies, waits for them, and re-layouts  31.3 us (12%)
  blocking collectives  3.89 us (1%)
    dot_general x28, matrix products, contract_rows(): lax.dot_general(left, right, (((0,), (0,)), ((), ())), precision=lax.Prec...  83.8 us
    mul x4, other arithmetic, place_rows(): load[:, :, None] * hot[:, None, :]  34.8 us
    all_to_all x2, starting transfers between devices, exchange_both(): parts = lax.all_to_all(parts, axis, split_axis=0, concat_axis=0, tiled=True)  24.8 us
    all_to_all x2, waiting for transfers between devices, exchange_both(): parts = lax.all_to_all(parts, axis, split_axis=0, concat_axis=0, tiled=True)  20.1 us
    mul x12, local copies, waits for them, and re-layouts, spread_rows(): layer_hot[:, :, None] * weight_x[:, None, :]  17.2 us
    ppermute x2, starting transfers between devices, extended_2(): before = lax.ppermute(last, axis, up)  13.4 us
    ppermute x2, waiting for transfers between devices, extended_2(): after = lax.ppermute(initial, axis, down)  12.4 us
    ppermute x2, starting transfers between devices, shifted(): return lax.ppermute(block, axis, route)  9.15 us
  transfers between devices with their start and end apart: 8, of which 6 were waited for; matrix products, arithmetic and copies ran while one was open for 2% of the time, Pallas kernels for 0%

commit v1 on v0

v1 whole, which is shorter than its diff:
```python
import functools

import jax
import jax.numpy as jnp
from jax import lax
from jax.experimental import pallas as pl
from jax.experimental.pallas import tpu as pltpu
from jax.sharding import PartitionSpec as P

F32 = jnp.float32
BF16 = jnp.bfloat16
MESH_ID = pl.DeviceIdType.MESH
VMEM_SPEC = pl.BlockSpec(memory_space=pltpu.VMEM)
SLOT = 64
TILES = 128
CHUNKS = 3
ROWS = 64
DEAD = 1000.0


def packed_iota(groups, shift):
    a = lax.broadcasted_iota(jnp.int32, (groups, 16, 128), 0)
    b = lax.broadcasted_iota(jnp.int32, (groups, 16, 128), 1)
    return (a * 16 + b + shift).astype(F32).astype(BF16)


def spread_row(row):
    return jnp.broadcast_to(row, (16, 128)).astype(BF16)[None]


def two_parts(x):
    hi = x.astype(BF16).astype(F32)
    return hi, x - hi


def dot_t(a, b):
    return lax.dot_general(a, b, (((1,), (1,)), ((), ())), preferred_element_type=F32)


def dot_n(a, b):
    return lax.dot_general(a, b, (((1,), (0,)), ((), ())), preferred_element_type=F32)


def rank_stage(length, tile_ref, d_ref, s_ref):
    i = lax.broadcasted_iota(jnp.int32, (256, 256), 0)
    j = lax.broadcasted_iota(jnp.int32, (256, 256), 1)
    before = (i < j).astype(F32).astype(BF16)
    every = jnp.ones((256, 256), BF16)
    tiles_id = lax.broadcasted_iota(jnp.int32, (TILES, 256), 0)
    lane = lax.broadcasted_iota(jnp.int32, (1, 256), 1)

    def step(k, offset):
        t = jnp.concatenate([tile_ref[pl.ds(2 * k, 1), :], tile_ref[pl.ds(2 * k + 1, 1), :]], axis=1)
        live = (lane + k * 256) < length
        t = jnp.where(live, t, -1)
        match = tiles_id == t
        hot = match.astype(F32)
        hot16 = hot.astype(BF16)
        within = dot_n(hot16, before)
        total = dot_n(hot16, every)
        rank = jnp.sum(jnp.where(match, within + offset, 0.0), axis=0, keepdims=True)
        c = jnp.floor(rank * (1.0 / SLOT))
        s = rank - c * SLOT
        d = jnp.where(live, c * TILES + t.astype(F32) - 192.0, DEAD)
        d_ref[pl.ds(2 * k, 1), :] = d[:, :128]
        d_ref[pl.ds(2 * k + 1, 1), :] = d[:, 128:]
        s_ref[pl.ds(2 * k, 1), :] = s[:, :128]
        s_ref[pl.ds(2 * k + 1, 1), :] = s[:, 128:]
        return offset + total

    lax.fori_loop(0, ROWS // 2, step, jnp.zeros((TILES, 256), F32))


def pack_stage(val_ref, frac_ref, cell_ref, layer_ref, d_ref, s_ref, acc_ref, out_ref):
    d_ids = packed_iota(24, -192)
    s_ids = packed_iota(4, 0)
    one = jnp.ones((1, 16, 128), BF16)
    zero = jnp.zeros((1, 16, 128), BF16)
    acc_ref[...] = jnp.zeros_like(acc_ref)
    per = 4

    def step(k, carry):
        lefts, highs, lows = [], [], []
        for q in range(per):
            r = k * per + q
            d = spread_row(d_ref[pl.ds(r, 1), :])
            s = spread_row(s_ref[pl.ds(r, 1), :])
            lefts.append(jnp.where(d_ids == d, one, zero).reshape(384, 128))
            mask = s_ids == s
            v = val_ref[pl.ds(r, 1), :]
            fx = frac_ref[0:1, pl.ds(pl.multiple_of(r * 128, 128), 128)]
            fy = frac_ref[1:2, pl.ds(pl.multiple_of(r * 128, 128), 128)]
            pos = layer_ref[pl.ds(r, 1), :] * 2048 + cell_ref[pl.ds(r, 1), :]
            pos_low = (pos & 255).astype(F32)
            pos_high = pos.astype(F32) - pos_low
            parts = [two_parts(v), (pos_high, pos_low), two_parts(fx), two_parts(fy)]
            for into, p in ((highs, 0), (lows, 1)):
                into.append(
                    jnp.concatenate(
                        [jnp.where(mask, spread_row(w[p]), zero).reshape(SLOT, 128) for w in parts],
                        axis=0,
                    )
                )
        left = jnp.concatenate(lefts, axis=1)
        acc_ref[...] += dot_t(left, jnp.concatenate(highs, axis=1)) + dot_t(
            left, jnp.concatenate(lows, axis=1)
        )
        return carry

    lax.fori_loop(0, ROWS // per, step, 0)
    for c in range(CHUNKS):
        for h in range(2):
            out_ref[:, 2 * c + h, :] = acc_ref[c * TILES : (c + 1) * TILES, h * 128 : (h + 1) * 128]


def pack_kernel(length_ref, val_ref, frac_ref, cell_ref, layer_ref, tile_ref, out_ref, d_ref, s_ref, acc_ref):
    rank_stage(length_ref[0], tile_ref, d_ref, s_ref)
    pack_stage(val_ref, frac_ref, cell_ref, layer_ref, d_ref, s_ref, acc_ref, out_ref)


def place_of(tx, ty):
    return tx // 8, (tx // 2) % 4, (tx % 2) * 2 + ty


def partner(tx, ty, off, sign):
    z, y, x = place_of(tx, ty)
    z = (z + sign * (off // 16) + 8) % 8
    y = (y + sign * ((off // 4) % 4) + 4) % 4
    x = (x + sign * (off % 4) + 4) % 4
    return z * 8 + y * 2 + x // 2, x % 2


def exchange_kernel(s_ref, r_ref, send_sem, recv_sem):
    tx = lax.axis_index("tx")
    ty = lax.axis_index("ty")
    me = tx * 2 + ty
    barrier = pltpu.get_barrier_semaphore()

    def greet(off, carry):
        px, py = partner(tx, ty, off, 1)
        pl.semaphore_signal(barrier, inc=1, device_id={"tx": px, "ty": py}, device_id_type=MESH_ID)
        return carry

    lax.fori_loop(1, TILES, greet, 0)
    pl.semaphore_wait(barrier, TILES - 1)

    def send(off, carry):
        px, py = partner(tx, ty, off, 1)
        pltpu.make_async_remote_copy(
            src_ref=s_ref.at[px * 2 + py],
            dst_ref=r_ref.at[me],
            send_sem=send_sem.at[off],
            recv_sem=recv_sem.at[off],
            device_id={"tx": px, "ty": py},
            device_id_type=MESH_ID,
        ).start()
        return carry

    lax.fori_loop(1, TILES, send, 0)
    r_ref[pl.ds(me, 1)] = s_ref[pl.ds(me, 1)]

    def finish(off, carry):
        px, py = partner(tx, ty, off, 1)
        qx, qy = partner(tx, ty, off, -1)
        copy = pltpu.make_async_remote_copy(
            src_ref=s_ref.at[px * 2 + py],
            dst_ref=r_ref.at[qx * 2 + qy],
            send_sem=send_sem.at[off],
            recv_sem=recv_sem.at[off],
            device_id={"tx": px, "ty": py},
            device_id_type=MESH_ID,
        )
        copy.wait_recv()
        copy.wait_send()
        return carry

    lax.fori_loop(1, TILES, finish, 0)


def spread_block(r_ref, first, acc_ref):
    lane = lax.broadcasted_iota(jnp.int32, (8, 128), 1)
    low = lane < SLOT
    x_ids = packed_iota(12, 0)
    y_ids = packed_iota(8, 0)
    rim_id = lax.broadcasted_iota(jnp.int32, (16, 128), 0)
    one = jnp.ones((1, 16, 128), BF16)
    zero = jnp.zeros((1, 16, 128), BF16)

    def both(j):
        a = r_ref[pl.ds(first, 8), j, :]
        b = r_ref[pl.ds(first + 8, 8), j, :]
        return jnp.where(low, a, pltpu.roll(b, SLOT, 1)), jnp.where(low, pltpu.roll(a, SLOT, 1), b)

    for c in range(CHUNKS):
        v, pos = both(2 * c)
        fx, fy = both(2 * c + 1)
        key = jnp.floor(pos * (1.0 / 128.0))
        cy = pos - key * 128.0
        v1 = v * fx
        v0 = v * (1.0 - fx)
        gy = 1.0 - fy
        q = [two_parts(u) for u in (v0 * gy, v0 * fy, v1 * gy, v1 * fy)]
        last = cy == 127.0
        rims = [[jnp.where(last, q[1][p], 0.0), jnp.where(last, q[3][p], 0.0)] for p in range(2)]
        rights, lefts = [], [[], []]
        for r in range(8):
            def row(u):
                return u[r : r + 1, :]
            rights.append(jnp.where(x_ids == spread_row(row(key)), one, zero).reshape(192, 128))
            here = spread_row(row(cy))
            m0 = y_ids == here
            m1 = y_ids == spread_row(row(cy) + 1.0)
            for p in range(2):
                pieces = []
                for a in range(2):
                    w0 = spread_row(row(q[2 * a][p]))
                    w1 = spread_row(row(q[2 * a + 1][p]))
                    pieces.append(jnp.where(m0, w0, jnp.where(m1, w1, zero)).reshape(128, 128))
                edge = jnp.where(
                    rim_id == 0,
                    jnp.broadcast_to(row(rims[p][0]), (16, 128)),
                    jnp.where(rim_id == 1, jnp.broadcast_to(row(rims[p][1]), (16, 128)), 0.0),
                ).astype(BF16)
                lefts[p].append(jnp.concatenate(pieces + [edge], axis=0))
        right = jnp.concatenate(rights, axis=1)
        acc_ref[...] += dot_t(jnp.concatenate(lefts[0], axis=1), right) + dot_t(
            jnp.concatenate(lefts[1], axis=1), right
        )


def spread_kernel(r_ref, base_ref, next_ref, rim_ref, acc_ref):
    acc_ref[...] = jnp.zeros_like(acc_ref)

    def step(k, carry):
        spread_block(r_ref, k * 16, acc_ref)
        return carry

    lax.fori_loop(0, 8, step, 0)
    base_ref[...] = acc_ref[0:128, :].T
    next_ref[...] = acc_ref[128:256, :].T
    rim_ref[...] = acc_ref[256:264, :]


def shifted(block, axis, distance):
    devices = range(lax.axis_size(axis))
    route = [(i - distance, i) for i in devices if i - distance in devices]
    return lax.ppermute(block, axis, route)


def of_everyone(x, axis):
    copies = jnp.broadcast_to(x, (lax.axis_size(axis), *x.shape))
    return jnp.sum(lax.all_to_all(copies, axis, split_axis=0, concat_axis=0, tiled=True), axis=0)


def extended_2(x, sides, width):
    for axis, dim in sides:
        size, length = (lax.axis_size(axis), x.shape[dim])
        up = [(i, (i + 1) % size) for i in range(size - 1)]
        down = [(j, i) for i, j in up]
        last = lax.slice_in_dim(x, length - width, length, axis=dim)
        initial = lax.slice_in_dim(x, 0, width, axis=dim)
        before = lax.ppermute(last, axis, up)
        after = lax.ppermute(initial, axis, down)
        x = jnp.concatenate([before, x, after], axis=dim)
    return x


def smooth(padded):
    along_x = 0.25 * padded[:, :, :-2, :] + 0.5 * padded[:, :, 1:-1, :] + 0.25 * padded[:, :, 2:, :]
    return 0.25 * along_x[:, :, :, :-2] + 0.5 * along_x[:, :, :, 1:-1] + 0.25 * along_x[:, :, :, 2:]


def body(obs_value, obs_frac, obs_cell, obs_layer, obs_tile, obs_length, ensemble):
    square = (ROWS, 128)
    packed = pl.pallas_call(
        pack_kernel,
        out_shape=jax.ShapeDtypeStruct((TILES, 6, 128), F32),
        in_specs=[pl.BlockSpec(memory_space=pltpu.SMEM)] + [VMEM_SPEC] * 5,
        out_specs=VMEM_SPEC,
        scratch_shapes=[pltpu.VMEM(square, F32), pltpu.VMEM(square, F32), pltpu.VMEM((384, 256), F32)],
    )(
        obs_length,
        obs_value.reshape(square),
        obs_frac,
        obs_cell.reshape(square),
        obs_layer.reshape(square),
        obs_tile.reshape(square),
    )
    got = pl.pallas_call(
        exchange_kernel,
        out_shape=jax.ShapeDtypeStruct((TILES, 6, 128), F32),
        in_specs=[VMEM_SPEC],
        out_specs=VMEM_SPEC,
        scratch_shapes=[pltpu.SemaphoreType.DMA((TILES,)), pltpu.SemaphoreType.DMA((TILES,))],
        compiler_params=pltpu.CompilerParams(collective_id=0, has_side_effects=True),
    )(packed)
    base, after, rims = pl.pallas_call(
        spread_kernel,
        out_shape=[
            jax.ShapeDtypeStruct((192, 128), F32),
            jax.ShapeDtypeStruct((192, 128), F32),
            jax.ShapeDtypeStruct((8, 192), F32),
        ],
        in_specs=[VMEM_SPEC],
        out_specs=[VMEM_SPEC] * 3,
        scratch_shapes=[pltpu.VMEM((272, 192), F32)],
    )(got)
    base = base.reshape(12, 16, 128)
    after = after.reshape(12, 16, 128)
    rim0 = rims[0].reshape(12, 16)
    rim1 = rims[1].reshape(12, 16)
    interior = base + jnp.pad(after[:, :15, :], ((0, 0), (1, 0), (0, 0)))
    east_rim = after[:, 15, :]
    north_rim = jnp.pad(rim0, ((0, 0), (0, 1))) + jnp.pad(rim1, ((0, 0), (1, 0)))
    from_south = shifted(north_rim, "ty", 1)
    interior = interior.at[:, :, 0].add(from_south[:, :16])
    east_rim = east_rim.at[:, 0].add(from_south[:, 16])
    from_west = shifted(east_rim, "tx", 1)
    interior = interior.at[:, 0, :].add(from_west)
    grad = of_everyone(interior, "mem")
    grad_slots = grad.reshape(6, 2, 16, 128)
    contrib = jnp.sum(ensemble * grad_slots[None], axis=1)
    padded = extended_2(contrib, (("tx", 2), ("ty", 3)), 1)
    return smooth(padded).astype(jnp.bfloat16)


def solution(mesh):
    placed = (
        P(("tx", "ty", "mem")),
        P(None, ("tx", "ty", "mem")),
        P(("tx", "ty", "mem")),
        P(("tx", "ty", "mem")),
        P(("tx", "ty", "mem")),
        P(("tx", "ty", "mem")),
        P("mem", None, None, "tx", "ty"),
    )
    return jax.shard_map(
        body, mesh=mesh, in_specs=placed, out_specs=P("mem", None, "tx", "ty"), check_vma=False
    )
```

time: 260 us -> 112 us (0.43)
  matrix products: 87 us -> 0 us
  Pallas kernels: 0 us -> 56.9 us
  other arithmetic: 49.7 us -> 3.37 us
  starting transfers between devices: 50.5 us -> 20.5 us
  local copies, waits for them, and re-layouts: 31.3 us -> 11 us
  waiting for transfers between devices: 34 us -> 15.3 us
    dot_general x29 -> x0, matrix products: 87 us -> none  [the longest x28 83.8 us: contract_rows(): lax.dot_general(left, right, (((0,), (0,)), ((), ())), precision=lax.Prec...]
    pallas_call x0 -> x3, Pallas kernels: none -> 56.9 us  [the longest x1 30.7 us: body(): pl.pallas_call(exchange_kernel, out_shape=jax.ShapeDtypeStruct((TILES, 6,...]
    mul x16 -> x0, other arithmetic: 37.9 us -> none  [the longest x4 34.8 us: place_rows(): load[:, :, None] * hot[:, None, :]]
    all_to_all x2 -> x0, starting transfers between devices: 24.8 us -> none  [exchange_both(): parts = lax.all_to_all(parts, axis, split_axis=0, concat_axis=0, tiled=True)]
    all_to_all x2 -> x0, waiting for transfers between devices: 20.1 us -> none  [exchange_both(): parts = lax.all_to_all(parts, axis, split_axis=0, concat_axis=0, tiled=True)]
    mul x12 -> x0, local copies, waits for them, and re-layouts: 17.2 us -> none  [spread_rows(): layer_hot[:, :, None] * weight_x[:, None, :]]
    dynamic_slice x40 -> x0, local copies, waits for them, and re-layouts: 6.93 us -> none  [the longest x4 5.2 us: place_rows(): hot = lax.dynamic_slice_in_dim(one_hot, start, send_block, 0)]
    convert_element_type x2 -> x0, other arithmetic: 4.94 us -> none  [the longest x1 4.93 us: body(): one_hot = ((obs_tile[:, None] == jnp.arange(tile_count, dtype=jnp.int32)[...]
  transfers between devices with their start and end apart: 8 -> 6, of which waited for: 6 -> 3; matrix products, arithmetic and copies ran while one was open for 2% -> 6% of each run, Pallas kernels for 0% -> 0%
where the time goes in v1:
time: 112 us
  Pallas kernels  56.9 us (51%)
  starting transfers between devices  20.5 us (18%)
  waiting for transfers between devices  15.3 us (14%)
  local copies, waits for them, and re-layouts  11 us (10%)
  blocking collectives  3.89 us (3%)
  other arithmetic  3.37 us (3%)
    pallas_call x1, Pallas kernels, body(): pl.pallas_call(exchange_kernel, out_shape=jax.ShapeDtypeStruct((TILES, 6,...  30.7 us
    pallas_call x1, Pallas kernels, body(): pl.pallas_call(pack_kernel, out_shape=jax.ShapeDtypeStruct((TILES, 6, 128...  15.1 us
    ppermute x2, waiting for transfers between devices, extended_2(): after = lax.ppermute(initial, axis, down)  12.2 us
    pallas_call x1, Pallas kernels, body(): pl.pallas_call(spread_kernel, out_shape=[jax.ShapeDtypeStruct((192, 128),...  11.2 us
    ppermute x2, starting transfers between devices, extended_2(): before = lax.ppermute(last, axis, up)  9.53 us
    ppermute x2, starting transfers between devices, shifted(): return lax.ppermute(block, axis, route)  7.78 us
    all_to_all x1, blocking collectives, of_everyone(): lax.all_to_all(copies, axis, split_axis=0, concat_axis=0, tiled=True)  3.89 us
    ppermute x2, starting transfers between devices, extended_2(): after = lax.ppermute(initial, axis, down)  3.2 us
  transfers between devices with their start and end apart: 6, of which 3 were waited for; matrix products, arithmetic and copies ran while one was open for 6% of the time, Pallas kernels for 0%

profile of v1, /device:TPU:28, one launch (start us, length us, event | category | flops | bytes accessed | tf_op | source)
XLA Modules:
  0.0 111.8 jit_solution(16263085745692966916)
XLA Ops:
  0.7 15.1 %shard_map.73.s_ref = f32[128,6,128]{2,1,0:T(8,128)} custom-call(s32[1]{0:T(128)S(6)} %copy.61.length_ref, f32[64,128]{1,0:T(8,128)} %bitcast.25, f32[2,8192]{1,0:T(2,128)} %frac_ref.1, s32[64,128]{1,0:T(8,128)} %bitcast.26, s32[64,128]{1,0:T(8,128)} %bitcast.27, s32[64,128]{1,0:T(8,128)} %bitcast.28), custom_call_target="tpu_custom_call" | custom-call | tf_op jit(solution)/shard_map/pallas_call | solution.py:275
  15.7 30.7 %shard_map.74.r_ref = f32[128,6,128]{2,1,0:T(8,128)} custom-call(f32[128,6,128]{2,1,0:T(8,128)} %shard_map.73.s_ref), custom_call_target="tpu_custom_call" | custom-call | tf_op jit(solution)/shard_map/pallas_call | solution.py:289
  46.4 11.2 %shard_map.75 = (f32[192,128]{1,0:T(8,128)}, f32[192,128]{1,0:T(8,128)}, f32[8,192]{1,0:T(8,128)}) custom-call(f32[128,6,128]{2,1,0:T(8,128)} %shard_map.74.r_ref), custom_call_target="tpu_custom_call" | custom-call | tf_op jit(solution)/shard_map/pallas_call | solution.py:297
  57.6 0.8 slice_reduce_fusion.1
  58.4 0.1 reshape_squeeze.6
  58.5 0.1 copy.40
  58.5 0.1 reshape_squeeze.7
  58.6 0.1 copy.41
  58.7 3.1 %collective-permute-start = (f32[12,17]{0,1:T(8,128)S(1)}, f32[12,17]{0,1:T(8,128)S(1)}, u32[]{:S(2)}, u32[]{:S(2)}) collective-permute-start(f32[12,17]{0,1:T(8,128)S(1)} %pad_add_fusion.1), channel_id=1, source_target_pairs={{0,2},{1,3},{4,6},{5,7},{8,10},{9,11},{12,14},{13,15},{16,18},{17,... | collective-permute-start | bytes 2456 | tf_op jit(solution)/shard_map/ppermute | solution.py:247
  61.9 1.4 %copy.55 = f32[12,15,128]{0,1,2:T(8,128)S(1)} copy(f32[12,15,128]{2,1,0:T(8,128)} %bitcast.19) | data formatting | bytes 184320
  63.3 1.4 %copy.39 = f32[12,16,128]{0,1,2:T(8,128)S(1)} copy(f32[12,16,128]{2,1,0:T(8,128)} %bitcast.22) | data formatting | bytes 196608 | tf_op jit(solution)/shard_map/reshape | solution.py:308
  64.7 0.2 pad_add_fusion
  64.9 0.0 copy-start
  64.9 0.9 slice.134
  65.9 0.8 slice.133
  66.7 0.1 copy.57
  66.8 0.1 copy.56
  66.9 0.6 compare_reduce_fusion
  67.5 0.0 collective-permute-done
  67.5 0.6 broadcast_select_fusion
  68.2 4.6 %collective-permute-start.1 = (f32[12,128]{0,1:T(8,128)S(1)}, f32[12,128]{0,1:T(8,128)S(1)}, u32[]{:S(2)}, u32[]{:S(2)}) collective-permute-start(f32[12,128]{0,1:T(8,128)S(1)} %scatter-add.11), channel_id=1, source_target_pairs={{0,4},{4,8},{8,12},{12,16},{16,20},{20,24},{24,28},{28,32},{32,36}... | collective-permute-start | bytes 18440 | tf_op jit(solution)/shard_map/ppermute | solution.py:247
  72.8 3.0 %collective-permute-done.1 = f32[12,128]{0,1:T(8,128)S(1)} collective-permute-done((f32[12,128]{0,1:T(8,128)S(1)}, f32[12,128]{0,1:T(8,128)S(1)}, u32[]{:S(2)}, u32[]{:S(2)}) %collective-permute-start.1) | collective-permute-done | bytes 6176 | tf_op jit(solution)/shard_map/ppermute | solution.py:247
  75.9 0.1 slice_add_fusion
  75.9 1.5 %scatter-add.14 = f32[12,16,128]{0,1,2:T(8,128)S(1)} dynamic-update-slice(f32[12,16,128]{0,1,2:T(8,128)S(1)} %fusion.6, f32[12,1,128]{0,1,2:T(1,128)S(1)} %slice_add_fusion, s32[]{:T(128)} %constant.86.clone.1, s32[]{:T(128)} %constant.86.clone.1, s32[]{:T(128)} %constant.86.clone.1) | dynamic-update-slice | bytes 12292 | tf_op jit(solution)/shard_map/scatter-add | solution.py:319
  77.5 0.5 copy.44
  77.9 3.9 %all_to_all.5 = f32[2,12,16,128]{3,2,1,0:T(8,128)S(1)} all-to-all(f32[2,12,16,128]{3,2,1,0:T(8,128)S(1)} %broadcast_in_dim.3), channel_id=1, replica_groups=mesh['tx'=64,'ty'=2,'mem'=2] {'mem'}, dimensions={0} | all-to-all | bytes 393216 | tf_op jit(solution)/shard_map/all_to_all | solution.py:252
  81.8 0.0 copy-done
  81.9 0.4 multiply_reduce_fusion
  82.3 0.1 fusion.8
  82.3 7.6 %collective-permute-start.2 = (f32[40,2,1,128]{3,0,2,1:T(8,128)S(1)}, f32[40,2,1,128]{3,0,2,1:T(8,128)S(1)}, u32[]{:S(2)}, u32[]{:S(2)}) collective-permute-start(f32[40,2,1,128]{3,0,2,1:T(8,128)S(1)} %copy.45), channel_id=1, source_target_pairs={{0,4},{4,8},{8,12},{12,16},{16,20},{20,24},{24,28},{28,32},{32,36}... | collective-permute-start | bytes 122888 | tf_op jit(solution)/shard_map/ppermute | solution.py:262
  90.0 1.9 %collective-permute-start.3 = (f32[40,2,1,128]{3,0,2,1:T(8,128)S(1)}, f32[40,2,1,128]{3,0,2,1:T(8,128)S(1)}, u32[]{:S(2)}, u32[]{:S(2)}) collective-permute-start(f32[40,2,1,128]{3,0,2,1:T(8,128)S(1)} %copy.46), channel_id=1, source_target_pairs={{4,0},{8,4},{12,8},{16,12},{20,16},{24,20},{28,24},{32,28},{36,32}... | collective-permute-start | bytes 122888 | tf_op jit(solution)/shard_map/ppermute | solution.py:263
  91.9 0.0 collective-permute-done.2
  92.0 8.4 %collective-permute-done.3 = f32[40,2,1,128]{3,0,2,1:T(8,128)S(1)} collective-permute-done((f32[40,2,1,128]{3,0,2,1:T(8,128)S(1)}, f32[40,2,1,128]{3,0,2,1:T(8,128)S(1)}, u32[]{:S(2)}, u32[]{:S(2)}) %collective-permute-start.3) | collective-permute-done | bytes 40992 | tf_op jit(solution)/shard_map/ppermute | solution.py:263
  100.5 0.2 pad_maximum_fusion.1
  100.6 0.3 fusion.7
  101.0 0.5 copy.49
  101.4 1.9 %collective-permute-start.4 = (f32[40,2,18,1]{0,2,3,1:T(8,128)S(1)}, f32[40,2,18,1]{0,2,3,1:T(8,128)S(1)}, u32[]{:S(2)}, u32[]{:S(2)}) collective-permute-start(f32[40,2,18,1]{0,2,3,1:T(8,128)S(1)} %copy.49), channel_id=1, source_target_pairs={{0,2},{1,3},{4,6},{5,7},{8,10},{9,11},{12,14},{13,15},{16,18},{17,... | collective-permute-start | bytes 17288 | tf_op jit(solution)/shard_map/ppermute | solution.py:262
  103.3 0.5 copy.50
  103.8 1.3 %collective-permute-start.5 = (f32[40,2,18,1]{0,2,3,1:T(8,128)S(1)}, f32[40,2,18,1]{0,2,3,1:T(8,128)S(1)}, u32[]{:S(2)}, u32[]{:S(2)}) collective-permute-start(f32[40,2,18,1]{0,2,3,1:T(8,128)S(1)} %copy.50), channel_id=1, source_target_pairs={{2,0},{3,1},{6,4},{7,5},{10,8},{11,9},{14,12},{15,13},{18,16},{19,... | collective-permute-start | bytes 17288 | tf_op jit(solution)/shard_map/ppermute | solution.py:263
  105.1 0.2 copy.52
  105.3 0.0 collective-permute-done.4
  105.3 0.3 copy.51
  105.7 3.8 %collective-permute-done.5 = f32[40,2,18,1]{0,2,3,1:T(8,128)S(1)} collective-permute-done((f32[40,2,18,1]{0,2,3,1:T(8,128)S(1)}, f32[40,2,18,1]{0,2,3,1:T(8,128)S(1)}, u32[]{:S(2)}, u32[]{:S(2)}) %collective-permute-start.5) | collective-permute-done | bytes 5792 | tf_op jit(solution)/shard_map/ppermute | solution.py:263
  109.5 0.3 copy.53
  109.8 0.6 pad_maximum_fusion
  110.5 0.2 fusion
  110.7 0.4 fusion.3
  111.1 0.8 copy.54
  (9 shorter events, 0.2 us)
Async XLA Ops:
  58.7 8.8 %collective-permute-start = (f32[12,17]{0,1:T(8,128)S(1)}, f32[12,17]{0,1:T(8,128)S(1)}, u32[]{:S(2)}, u32[]{:S(2)}) collective-permute-start(f32[12,17]{0,1:T(8,128)S(1)} %pad_add_fusion.1), channel_id=1, source_target_pairs={{0,2},{1,3},{4,6},{5,7},{8,10},{9,11},{12,14},{13,15},{16,18},{17,... | collective-permute-start | bytes 2456 | tf_op jit(solution)/shard_map/ppermute | solution.py:247
  64.9 16.9 %copy-start = (bf16[40,6,2,16,128]{4,3,2,1,0:T(8,128)(2,1)S(1)}, bf16[40,6,2,16,128]{4,3,2,1,0:T(8,128)(2,1)}, u32[]{:S(2)}) copy-start(bf16[40,6,2,16,128]{4,3,2,1,0:T(8,128)(2,1)} %param.19) | copy-start | bytes 5898244
  68.2 7.7 %collective-permute-start.1 = (f32[12,128]{0,1:T(8,128)S(1)}, f32[12,128]{0,1:T(8,128)S(1)}, u32[]{:S(2)}, u32[]{:S(2)}) collective-permute-start(f32[12,128]{0,1:T(8,128)S(1)} %scatter-add.11), channel_id=1, source_target_pairs={{0,4},{4,8},{8,12},{12,16},{16,20},{20,24},{24,28},{28,32},{32,36}... | collective-permute-start | bytes 18440 | tf_op jit(solution)/shard_map/ppermute | solution.py:247
  82.3 9.6 %collective-permute-start.2 = (f32[40,2,1,128]{3,0,2,1:T(8,128)S(1)}, f32[40,2,1,128]{3,0,2,1:T(8,128)S(1)}, u32[]{:S(2)}, u32[]{:S(2)}) collective-permute-start(f32[40,2,1,128]{3,0,2,1:T(8,128)S(1)} %copy.45), channel_id=1, source_target_pairs={{0,4},{4,8},{8,12},{12,16},{16,20},{20,24},{24,28},{28,32},{32,36}... | collective-permute-start | bytes 122888 | tf_op jit(solution)/shard_map/ppermute | solution.py:262
  90.0 10.4 %collective-permute-start.3 = (f32[40,2,1,128]{3,0,2,1:T(8,128)S(1)}, f32[40,2,1,128]{3,0,2,1:T(8,128)S(1)}, u32[]{:S(2)}, u32[]{:S(2)}) collective-permute-start(f32[40,2,1,128]{3,0,2,1:T(8,128)S(1)} %copy.46), channel_id=1, source_target_pairs={{4,0},{8,4},{12,8},{16,12},{20,16},{24,20},{28,24},{32,28},{36,32}... | collective-permute-start | bytes 122888 | tf_op jit(solution)/shard_map/ppermute | solution.py:263
  101.4 3.9 %collective-permute-start.4 = (f32[40,2,18,1]{0,2,3,1:T(8,128)S(1)}, f32[40,2,18,1]{0,2,3,1:T(8,128)S(1)}, u32[]{:S(2)}, u32[]{:S(2)}) collective-permute-start(f32[40,2,18,1]{0,2,3,1:T(8,128)S(1)} %copy.49), channel_id=1, source_target_pairs={{0,2},{1,3},{4,6},{5,7},{8,10},{9,11},{12,14},{13,15},{16,18},{17,... | collective-permute-start | bytes 17288 | tf_op jit(solution)/shard_map/ppermute | solution.py:262
  103.8 5.7 %collective-permute-start.5 = (f32[40,2,18,1]{0,2,3,1:T(8,128)S(1)}, f32[40,2,18,1]{0,2,3,1:T(8,128)S(1)}, u32[]{:S(2)}, u32[]{:S(2)}) collective-permute-start(f32[40,2,18,1]{0,2,3,1:T(8,128)S(1)} %copy.50), channel_id=1, source_target_pairs={{2,0},{3,1},{6,4},{7,5},{10,8},{11,9},{14,12},{15,13},{18,16},{19,... | collective-permute-start | bytes 17288 | tf_op jit(solution)/shard_map/ppermute | solution.py:263

commit v2 on v1

--- a/solution.py
+++ b/solution.py
@@ -113,11 +113,6 @@
             out_ref[:, 2 * c + h, :] = acc_ref[c * TILES : (c + 1) * TILES, h * 128 : (h + 1) * 128]
 
 
-def pack_kernel(length_ref, val_ref, frac_ref, cell_ref, layer_ref, tile_ref, out_ref, d_ref, s_ref, acc_ref):
-    rank_stage(length_ref[0], tile_ref, d_ref, s_ref)
-    pack_stage(val_ref, frac_ref, cell_ref, layer_ref, d_ref, s_ref, acc_ref, out_ref)
-
-
 def place_of(tx, ty):
     return tx // 8, (tx // 2) % 4, (tx % 2) * 2 + ty
 
@@ -128,53 +123,6 @@
     y = (y + sign * ((off // 4) % 4) + 4) % 4
     x = (x + sign * (off % 4) + 4) % 4
     return z * 8 + y * 2 + x // 2, x % 2
-
-
-def exchange_kernel(s_ref, r_ref, send_sem, recv_sem):
-    tx = lax.axis_index("tx")
-    ty = lax.axis_index("ty")
-    me = tx * 2 + ty
-    barrier = pltpu.get_barrier_semaphore()
-
-    def greet(off, carry):
-        px, py = partner(tx, ty, off, 1)
-        pl.semaphore_signal(barrier, inc=1, device_id={"tx": px, "ty": py}, device_id_type=MESH_ID)
-        return carry
-
-    lax.fori_loop(1, TILES, greet, 0)
-    pl.semaphore_wait(barrier, TILES - 1)
-
-    def send(off, carry):
-        px, py = partner(tx, ty, off, 1)
-        pltpu.make_async_remote_copy(
-            src_ref=s_ref.at[px * 2 + py],
-            dst_ref=r_ref.at[me],
-            send_sem=send_sem.at[off],
-            recv_sem=recv_sem.at[off],
-            device_id={"tx": px, "ty": py},
-            device_id_type=MESH_ID,
-        ).start()
-        return carry
-
-    lax.fori_loop(1, TILES, send, 0)
-    r_ref[pl.ds(me, 1)] = s_ref[pl.ds(me, 1)]
-
-    def finish(off, carry):
-        px, py = partner(tx, ty, off, 1)
-        qx, qy = partner(tx, ty, off, -1)
-        copy = pltpu.make_async_remote_copy(
-            src_ref=s_ref.at[px * 2 + py],
-            dst_ref=r_ref.at[qx * 2 + qy],
-            send_sem=send_sem.at[off],
-            recv_sem=recv_sem.at[off],
-            device_id={"tx": px, "ty": py},
-            device_id_type=MESH_ID,
-        )
-        copy.wait_recv()
-        copy.wait_send()
-        return carry
-
-    lax.fori_loop(1, TILES, finish, 0)
 
 
 def spread_block(r_ref, first, acc_ref):
@@ -228,56 +176,267 @@
         )
 
 
-def spread_kernel(r_ref, base_ref, next_ref, rim_ref, acc_ref):
-    acc_ref[...] = jnp.zeros_like(acc_ref)
-
-    def step(k, carry):
-        spread_block(r_ref, k * 16, acc_ref)
-        return carry
-
-    lax.fori_loop(0, 8, step, 0)
-    base_ref[...] = acc_ref[0:128, :].T
-    next_ref[...] = acc_ref[128:256, :].T
-    rim_ref[...] = acc_ref[256:264, :]
-
-
-def shifted(block, axis, distance):
-    devices = range(lax.axis_size(axis))
-    route = [(i - distance, i) for i in devices if i - distance in devices]
-    return lax.ppermute(block, axis, route)
-
-
-def of_everyone(x, axis):
-    copies = jnp.broadcast_to(x, (lax.axis_size(axis), *x.shape))
-    return jnp.sum(lax.all_to_all(copies, axis, split_axis=0, concat_axis=0, tiled=True), axis=0)
-
-
-def extended_2(x, sides, width):
-    for axis, dim in sides:
-        size, length = (lax.axis_size(axis), x.shape[dim])
-        up = [(i, (i + 1) % size) for i in range(size - 1)]
-        down = [(j, i) for i, j in up]
-        last = lax.slice_in_dim(x, length - width, length, axis=dim)
-        initial = lax.slice_in_dim(x, 0, width, axis=dim)
-        before = lax.ppermute(last, axis, up)
-        after = lax.ppermute(initial, axis, down)
-        x = jnp.concatenate([before, x, after], axis=dim)
-    return x
-
-
-def smooth(padded):
-    along_x = 0.25 * padded[:, :, :-2, :] + 0.5 * padded[:, :, 1:-1, :] + 0.25 * padded[:, :, 2:, :]
-    return 0.25 * along_x[:, :, :, :-2] + 0.5 * along_x[:, :, :, 1:-1] + 0.25 * along_x[:, :, :, 2:]
+def order_of(i):
+    return (i % 8) * 16 + i // 8
+
+
+def remote(src, dst, send_sem, recv_sem, where):
+    return pltpu.make_async_remote_copy(
+        src_ref=src, dst_ref=dst, send_sem=send_sem, recv_sem=recv_sem, device_id=where, device_id_type=MESH_ID
+    )
+
+
+def edge_columns(ens_ref, edge, out_ref):
+    k = lax.broadcasted_iota(jnp.int32, (1024, 128), 0)
+    col = lax.broadcasted_iota(jnp.int32, (1024, 128), 1)
+    total = jnp.zeros((192, 128), F32)
+    for g in range(5):
+        left = jnp.concatenate([ens_ref[8 * g + m] for m in range(8)], axis=1)
+        pick = ((k % 128 == edge) & (k // 128 + 8 * g == col)).astype(F32).astype(BF16)
+        total = total + dot_n(left, pick)
+    out_ref[...] = total
+
+
+def all_kernel(
+    length_ref, val_ref, frac_ref, cell_ref, layer_ref, tile_ref, ens_hbm, out_ref,
+    d_ref, s_ref, acc_ref, sbuf, rbuf, grid_ref, ens_ref, col_ref,
+    part_buf, part_got, next_buf, east_buf, east_got, north_buf, north_got, corner_buf, corner_got,
+    g_ref, c_ref, f_ref, xe_buf, xe_got, ce_buf, ce_got, cc_buf, cc_got, hx_ref, hy_ref,
+    ens_sem, send_sem, recv_sem, send1, recv1, send2, recv2,
+):
+    tx = lax.axis_index("tx")
+    ty = lax.axis_index("ty")
+    mem = lax.axis_index("mem")
+    n_tx = lax.axis_size("tx")
+    east = lax.rem(tx + 1, n_tx)
+    west = lax.rem(tx + n_tx - 1, n_tx)
+    over = 1 - ty
+    twin = 1 - mem
+    barrier = pltpu.get_barrier_semaphore()
+
+    def greet(i, carry):
+        px, py = partner(tx, ty, order_of(i), 1)
+        pl.semaphore_signal(barrier, inc=1, device_id={"tx": px, "ty": py, "mem": mem}, device_id_type=MESH_ID)
+        return carry
+
+    lax.fori_loop(1, TILES, greet, 0)
+    for px, py in ((tx, ty), (west, ty), (tx, over), (west, over)):
+        pl.semaphore_signal(barrier, inc=1, device_id={"tx": px, "ty": py, "mem": twin}, device_id_type=MESH_ID)
+    ens_copy = pltpu.make_async_copy(ens_hbm, ens_ref, ens_sem)
+    ens_copy.start()
+
+    rank_stage(length_ref[0], tile_ref, d_ref, s_ref)
+    pack_stage(val_ref, frac_ref, cell_ref, layer_ref, d_ref, s_ref, acc_ref, sbuf)
+
+    pl.semaphore_wait(barrier, TILES - 1 + 4)
+
+    def message(i):
+        px, py = partner(tx, ty, order_of(i), 1)
+        return remote(
+            sbuf.at[px * 2 + py], rbuf.at[i], send_sem.at[i], recv_sem.at[i], {"tx": px, "ty": py, "mem": mem}
+        )
+
+    def send(i, carry):
+        message(i).start()
+        return carry
+
+    lax.fori_loop(1, TILES, send, 0)
+    rbuf[pl.ds(0, 1)] = sbuf[pl.ds(tx * 2 + ty, 1)]
+    edge = (1 - ty) * 127
+    ens_copy.wait()
+    edge_columns(ens_ref, edge, col_ref)
+
+    grid_ref[...] = jnp.zeros_like(grid_ref)
+
+    def arrive(i, carry):
+        message(i).wait_recv()
+        return carry
+
+    def gather(k, carry):
+        lax.fori_loop(jnp.maximum(k * 16, 1), k * 16 + 16, arrive, 0)
+        spread_block(rbuf, k * 16, grid_ref)
+        return carry
+
+    lax.fori_loop(0, 8, gather, 0)
+
+    row = lax.broadcasted_iota(jnp.int32, (192, 128), 0)
+    x_first = (row % 16) == 0
+    lane192 = lax.broadcasted_iota(jnp.int32, (192, 128), 1)
+    lane256 = lax.broadcasted_iota(jnp.int32, (8, 256), 1)
+    row8 = lax.broadcasted_iota(jnp.int32, (8, 256), 0)
+    after = grid_ref[128:256, :].T
+    mine = grid_ref[0:128, :].T + jnp.where(x_first, 0.0, pltpu.roll(after, 1, 0))
+    part_buf[...] = mine
+    next_buf[...] = after
+    east_buf[...] = next_buf[pl.ds(15, 12, stride=16), :]
+    pad = jnp.zeros((8, 64), F32)
+    rim0 = jnp.concatenate([jnp.broadcast_to(grid_ref[256:257, :], (8, 192)), pad], axis=1)
+    rim1 = jnp.concatenate([jnp.broadcast_to(grid_ref[257:258, :], (8, 192)), pad], axis=1)
+    top = row8 == 0
+    first256 = (lane256 % 16) == 0
+    north_buf[...] = jnp.where(top, rim0 + jnp.where(first256, 0.0, pltpu.roll(rim1, 1, 1)), 0.0)
+    corner_buf[...] = jnp.where(top & first256, pltpu.roll(rim1, 241, 1), 0.0)
+
+    first = [remote(part_buf, part_got, send1.at[0], recv1.at[0], {"tx": tx, "ty": ty, "mem": twin})]
+    for j in range(2):
+        first.append(remote(east_buf, east_got.at[mem], send1.at[1 + j], recv1.at[1 + mem], {"tx": east, "ty": ty, "mem": j}))
+        first.append(remote(north_buf, north_got.at[mem], send1.at[3 + j], recv1.at[3 + mem], {"tx": tx, "ty": over, "mem": j}))
+        first.append(remote(corner_buf, corner_got.at[mem], send1.at[5 + j], recv1.at[5 + mem], {"tx": east, "ty": over, "mem": j}))
+    for copy in first:
+        copy.start()
+    remote(part_buf, part_got, send1.at[0], recv1.at[0], {"tx": tx, "ty": ty, "mem": twin}).wait_recv()
+    for j in range(2):
+        remote(east_buf, east_got.at[j], send1.at[1 + j], recv1.at[1 + j], {"tx": east, "ty": ty, "mem": j}).wait_recv()
+        remote(north_buf, north_got.at[j], send1.at[3 + j], recv1.at[3 + j], {"tx": tx, "ty": over, "mem": j}).wait_recv()
+        remote(corner_buf, corner_got.at[j], send1.at[5 + j], recv1.at[5 + j], {"tx": east, "ty": over, "mem": j}).wait_recv()
+    has_west = jnp.where(tx > 0, 1.0, 0.0)
+    has_east = jnp.where(tx < n_tx - 1, 1.0, 0.0)
+    has_south = jnp.where(ty > 0, 1.0, 0.0)
+    rims = (north_got[0] + north_got[1] + (corner_got[0] + corner_got[1]) * has_west) * has_south
+    rims = jnp.concatenate([rims, jnp.zeros((120, 256), F32)], axis=0).T
+    wall = (east_got[0] + east_got[1]) * has_west
+    wall = jnp.broadcast_to(wall[:, None, :], (12, 16, 128)).reshape(192, 128)
+    g = part_buf[...] + part_got[...] + rims[0:192, :] + jnp.where(x_first, wall, 0.0)
+    g_ref[...] = g
+    gcol = jnp.sum(jnp.where(lane192 == edge, g, 0.0), axis=1, keepdims=True)
+    ce = jnp.zeros((32, 128), F32)
+    for t in range(6):
+        ce = ce + col_ref[t * 32 : t * 32 + 32, :] * gcol[t * 32 : t * 32 + 32, :]
+    ce_buf[...] = ce
+    for v in range(2):
+        cc_buf[0, v : v + 1, :] = ce[v * 16 : v * 16 + 1, :]
+        cc_buf[1, v : v + 1, :] = ce[v * 16 + 15 : v * 16 + 16, :]
+
+    def contract(m, carry):
+        total = jnp.zeros((32, 128), F32)
+        for t in range(6):
+            total = total + ens_ref[m, t * 32 : t * 32 + 32, :].astype(F32) * g_ref[t * 32 : t * 32 + 32, :]
+        c_ref[pl.ds(pl.multiple_of(m * 32, 32), 32), :] = total
+        return carry
+
+    lax.fori_loop(0, 40, contract, 0)
+    xe_buf[0] = c_ref[pl.ds(0, 80, stride=16), :]
+    xe_buf[1] = c_ref[pl.ds(15, 80, stride=16), :]
+
+    second = [
+        remote(xe_buf.at[0], xe_got.at[1], send2.at[0], recv2.at[1], {"tx": west, "ty": ty, "mem": mem}),
+        remote(xe_buf.at[1], xe_got.at[0], send2.at[1], recv2.at[0], {"tx": east, "ty": ty, "mem": mem}),
+        remote(ce_buf, ce_got, send2.at[2], recv2.at[2], {"tx": tx, "ty": over, "mem": mem}),
+        remote(cc_buf.at[0], cc_got.at[1], send2.at[3], recv2.at[4], {"tx": west, "ty": over, "mem": mem}),
+        remote(cc_buf.at[1], cc_got.at[0], send2.at[4], recv2.at[3], {"tx": east, "ty": over, "mem": mem}),
+    ]
+    for copy in second:
+        copy.start()
+
+    row32 = lax.broadcasted_iota(jnp.int32, (32, 128), 0) % 16
+    lane32 = lax.broadcasted_iota(jnp.int32, (32, 128), 1)
+
+    def along_x(c):
+        up = jnp.where(row32 == 0, 0.0, pltpu.roll(c, 1, 0))
+        down = jnp.where(row32 == 15, 0.0, pltpu.roll(c, 31, 0))
+        return 0.5 * c + 0.25 * (up + down)
+
+    def along_y(c, lane):
+        left = jnp.where(lane == 0, 0.0, pltpu.roll(c, 1, 1))
+        right = jnp.where(lane == 127, 0.0, pltpu.roll(c, 127, 1))
+        return 0.5 * c + 0.25 * (left + right)
+
+    def inside(m, carry):
+        at = pl.ds(pl.multiple_of(m * 32, 32), 32)
+        f_ref[at, :] = along_y(along_x(c_ref[at, :]), lane32)
+        return carry
+
+    lax.fori_loop(0, 40, inside, 0)
+
+    for copy in second:
+        copy.wait_send()
+    remote(xe_buf.at[0], xe_got.at[1], send2.at[0], recv2.at[1], {"tx": west, "ty": ty, "mem": mem}).wait_recv()
+    remote(xe_buf.at[1], xe_got.at[0], send2.at[1], recv2.at[0], {"tx": east, "ty": ty, "mem": mem}).wait_recv()
+    remote(ce_buf, ce_got, send2.at[2], recv2.at[2], {"tx": tx, "ty": over, "mem": mem}).wait_recv()
+    remote(cc_buf.at[0], cc_got.at[1], send2.at[3], recv2.at[4], {"tx": west, "ty": over, "mem": mem}).wait_recv()
+    remote(cc_buf.at[1], cc_got.at[0], send2.at[4], recv2.at[3], {"tx": east, "ty": over, "mem": mem}).wait_recv()
+
+    lane80 = lax.broadcasted_iota(jnp.int32, (80, 128), 1)
+    hx_ref[0] = along_y(xe_got[0], lane80) * (0.25 * has_west)
+    hx_ref[1] = along_y(xe_got[1], lane80) * (0.25 * has_east)
+    side = along_x(ce_got[...])
+    for v in range(2):
+        before = cc_got[0, v : v + 1, :] * (0.25 * has_west)
+        behind = cc_got[1, v : v + 1, :] * (0.25 * has_east)
+        here = lax.broadcasted_iota(jnp.int32, (32, 128), 0)
+        side = side + jnp.where(here == v * 16, before, 0.0) + jnp.where(here == v * 16 + 15, behind, 0.0)
+    hy_ref[...] = side * 0.25
+
+    def finish(m, carry):
+        at = pl.ds(pl.multiple_of(m * 32, 32), 32)
+        f = f_ref[at, :] + jnp.where(lane32 == edge, pltpu.roll(hy_ref[...], lax.rem(edge - m + 128, 128), 1), 0.0)
+        low, high = [], []
+        for v in range(2):
+            low.append(jnp.broadcast_to(hx_ref[0, pl.ds(2 * m + v, 1), :], (16, 128)))
+            high.append(jnp.broadcast_to(hx_ref[1, pl.ds(2 * m + v, 1), :], (16, 128)))
+        f = f + jnp.where(row32 == 0, jnp.concatenate(low, axis=0), 0.0)
+        f = f + jnp.where(row32 == 15, jnp.concatenate(high, axis=0), 0.0)
+        out_ref[m] = f.astype(BF16)
+        return carry
+
+    lax.fori_loop(0, 40, finish, 0)
+
+    for copy in first:
+        copy.wait_send()
+
+    def sent(i, carry):
+        message(i).wait_send()
+        return carry
+
+    lax.fori_loop(1, TILES, sent, 0)
 
 
 def body(obs_value, obs_frac, obs_cell, obs_layer, obs_tile, obs_length, ensemble):
     square = (ROWS, 128)
-    packed = pl.pallas_call(
-        pack_kernel,
-        out_shape=jax.ShapeDtypeStruct((TILES, 6, 128), F32),
-        in_specs=[pl.BlockSpec(memory_space=pltpu.SMEM)] + [VMEM_SPEC] * 5,
+    dma = pltpu.SemaphoreType.DMA
+    out = pl.pallas_call(
+        all_kernel,
+        out_shape=jax.ShapeDtypeStruct((40, 32, 128), BF16),
+        in_specs=[pl.BlockSpec(memory_space=pltpu.SMEM)] + [VMEM_SPEC] * 5 + [pl.BlockSpec(memory_space=pl.ANY)],
         out_specs=VMEM_SPEC,
-        scratch_shapes=[pltpu.VMEM(square, F32), pltpu.VMEM(square, F32), pltpu.VMEM((384, 256), F32)],
+        scratch_shapes=[
+            pltpu.VMEM(square, F32),
+            pltpu.VMEM(square, F32),
+            pltpu.VMEM((384, 256), F32),
+            pltpu.VMEM((TILES, 6, 128), F32),
+            pltpu.VMEM((TILES, 6, 128), F32),
+            pltpu.VMEM((272, 192), F32),
+            pltpu.VMEM((40, 192, 128), BF16),
+            pltpu.VMEM((192, 128), F32),
+            pltpu.VMEM((192, 128), F32),
+            pltpu.VMEM((192, 128), F32),
+            pltpu.VMEM((192, 128), F32),
+            pltpu.VMEM((12, 128), F32),
+            pltpu.VMEM((2, 12, 128), F32),
+            pltpu.VMEM((8, 256), F32),
+            pltpu.VMEM((2, 8, 256), F32),
+            pltpu.VMEM((8, 256), F32),
+            pltpu.VMEM((2, 8, 256), F32),
+            pltpu.VMEM((192, 128), F32),
+            pltpu.VMEM((1280, 128), F32),
+            pltpu.VMEM((1280, 128), F32),
+            pltpu.VMEM((2, 80, 128), F32),
+            pltpu.VMEM((2, 80, 128), F32),
+            pltpu.VMEM((32, 128), F32),
+            pltpu.VMEM((32, 128), F32),
+            pltpu.VMEM((2, 2, 128), F32),
+            pltpu.VMEM((2, 2, 128), F32),
+            pltpu.VMEM((2, 80, 128), F32),
+            pltpu.VMEM((32, 128), F32),
+            dma,
+            dma((TILES,)),
+            dma((TILES,)),
+            dma((7,)),
+            dma((7,)),
+            dma((5,)),
+            dma((5,)),
+        ],
+        compiler_params=pltpu.CompilerParams(collective_id=0, has_side_effects=True),
     )(
         obs_length,
         obs_value.reshape(square),
@@ -285,43 +444,9 @@
         obs_cell.reshape(square),
         obs_layer.reshape(square),
         obs_tile.reshape(square),
+        ensemble.reshape(40, 192, 128),
     )
-    got = pl.pallas_call(
-        exchange_kernel,
-        out_shape=jax.ShapeDtypeStruct((TILES, 6, 128), F32),
-        in_specs=[VMEM_SPEC],
-        out_specs=VMEM_SPEC,
-        scratch_shapes=[pltpu.SemaphoreType.DMA((TILES,)), pltpu.SemaphoreType.DMA((TILES,))],
-        compiler_params=pltpu.CompilerParams(collective_id=0, has_side_effects=True),
-    )(packed)
-    base, after, rims = pl.pallas_call(
-        spread_kernel,
-        out_shape=[
-            jax.ShapeDtypeStruct((192, 128), F32),
-            jax.ShapeDtypeStruct((192, 128), F32),
-            jax.ShapeDtypeStruct((8, 192), F32),
-        ],
-        in_specs=[VMEM_SPEC],
-        out_specs=[VMEM_SPEC] * 3,
-        scratch_shapes=[pltpu.VMEM((272, 192), F32)],
-    )(got)
-    base = base.reshape(12, 16, 128)
-    after = after.reshape(12, 16, 128)
-    rim0 = rims[0].reshape(12, 16)
-    rim1 = rims[1].reshape(12, 16)
-    interior = base + jnp.pad(after[:, :15, :], ((0, 0), (1, 0), (0, 0)))
-    east_rim = after[:, 15, :]
-    north_rim = jnp.pad(rim0, ((0, 0), (0, 1))) + jnp.pad(rim1, ((0, 0), (1, 0)))
-    from_south = shifted(north_rim, "ty", 1)
-    interior = interior.at[:, :, 0].add(from_south[:, :16])
-    east_rim = east_rim.at[:, 0].add(from_south[:, 16])
-    from_west = shifted(east_rim, "tx", 1)
-    interior = interior.at[:, 0, :].add(from_west)
-    grad = of_everyone(interior, "mem")
-    grad_slots = grad.reshape(6, 2, 16, 128)
-    contrib = jnp.sum(ensemble * grad_slots[None], axis=1)
-    padded = extended_2(contrib, (("tx", 2), ("ty", 3)), 1)
-    return smooth(padded).astype(jnp.bfloat16)
+    return out.reshape(40, 2, 16, 128)
 
 
 def solution(mesh):

time: 112 us -> 64.8 us (0.58)
  the two profiles are of different devices: /device:TPU:28 before, /device:TPU:1 now
where the time goes in v2:
time: 64.8 us; the launch traced here: 64.6 us
  Pallas kernels  62.2 us (96%)
  local copies, waits for them, and re-layouts  1.72 us (3%)
  between operations  0.66 us (1%)
    pallas_call x1, Pallas kernels, body(): pl.pallas_call(all_kernel, out_shape=jax.ShapeDtypeStruct((40, 32, 128),...  62.2 us
    unnamed x1, local copies, waits for them, and re-layouts  1.72 us

profile of v2, /device:TPU:1, one launch (start us, length us, event | category | flops | bytes accessed | tf_op | source)
XLA Modules:
  0.0 64.6 jit_solution(8339109976266491819)
XLA Ops:
  0.7 62.2 %shard_map.73 = bf16[40,32,128]{2,1,0:T(8,128)(2,1)} custom-call(s32[1]{0:T(128)S(6)} %copy.9.length_ref, f32[64,128]{1,0:T(8,128)} %bitcast.8, f32[2,8192]{1,0:T(2,128)} %frac_ref.1, s32[64,128]{1,0:T(8,128)} %bitcast.9, s32[64,128]{1,0:T(8,128)} %bitcast.10, s32[64,128]{1,0:T(8,128)} %bitcast.11, bf16[40,192,128]{2,1,0:T(8,128)(2,1)} %bitcast.6), custom_call_target="tpu_custom_call" | custom-call | tf_op jit(solution)/shard_map/pallas_call | solution.py:397
  62.9 1.7 %copy.10 = bf16[40,2,16,128]{3,2,1,0:T(8,128)(2,1)} copy(bf16[40,2,16,128]{3,2,1,0:T(8,128)(2,1)} %bitcast.7) | data formatting | bytes 655360

commit v3 on v2

--- a/solution.py
+++ b/solution.py
@@ -42,51 +42,47 @@
 
 
 def rank_stage(length, tile_ref, d_ref, s_ref):
-    i = lax.broadcasted_iota(jnp.int32, (256, 256), 0)
-    j = lax.broadcasted_iota(jnp.int32, (256, 256), 1)
-    before = (i < j).astype(F32).astype(BF16)
-    every = jnp.ones((256, 256), BF16)
-    tiles_id = lax.broadcasted_iota(jnp.int32, (TILES, 256), 0)
-    lane = lax.broadcasted_iota(jnp.int32, (1, 256), 1)
+    i = lax.broadcasted_iota(jnp.int32, (128, 256), 0)
+    j = lax.broadcasted_iota(jnp.int32, (128, 256), 1)
+    before = jnp.where((i < j) | (j >= 128), 1.0, 0.0).astype(BF16)
+    tiles_id = lax.broadcasted_iota(jnp.int32, (TILES, 128), 0)
+    lane = lax.broadcasted_iota(jnp.int32, (1, 128), 1)
+    per = 4
 
     def step(k, offset):
-        t = jnp.concatenate([tile_ref[pl.ds(2 * k, 1), :], tile_ref[pl.ds(2 * k + 1, 1), :]], axis=1)
-        live = (lane + k * 256) < length
-        t = jnp.where(live, t, -1)
-        match = tiles_id == t
-        hot = match.astype(F32)
-        hot16 = hot.astype(BF16)
-        within = dot_n(hot16, before)
-        total = dot_n(hot16, every)
-        rank = jnp.sum(jnp.where(match, within + offset, 0.0), axis=0, keepdims=True)
-        c = jnp.floor(rank * (1.0 / SLOT))
-        s = rank - c * SLOT
-        d = jnp.where(live, c * TILES + t.astype(F32) - 192.0, DEAD)
-        d_ref[pl.ds(2 * k, 1), :] = d[:, :128]
-        d_ref[pl.ds(2 * k + 1, 1), :] = d[:, 128:]
-        s_ref[pl.ds(2 * k, 1), :] = s[:, :128]
-        s_ref[pl.ds(2 * k + 1, 1), :] = s[:, 128:]
-        return offset + total
-
-    lax.fori_loop(0, ROWS // 2, step, jnp.zeros((TILES, 256), F32))
+        for q in range(per):
+            r = k * per + q
+            t = tile_ref[pl.ds(r, 1), :]
+            live = (lane + r * 128) < length
+            t = jnp.where(live, t, -1)
+            match = tiles_id == t
+            both = dot_n(jnp.where(match, 1.0, 0.0).astype(BF16), before)
+            rank = jnp.sum(jnp.where(match, both[:, :128] + offset, 0.0), axis=0, keepdims=True)
+            offset = offset + both[:, 128:]
+            c = jnp.floor(rank * (1.0 / SLOT))
+            tf = t.astype(F32)
+            t4 = jnp.floor(tf * 0.25)
+            d_ref[pl.ds(r, 1), :] = jnp.where(live, c * 32.0 + t4, DEAD)
+            s_ref[pl.ds(r, 1), :] = (tf - 4.0 * t4) * SLOT + (rank - c * SLOT)
+        return offset
+
+    lax.fori_loop(0, ROWS // per, step, jnp.zeros((TILES, 128), F32))
 
 
 def pack_stage(val_ref, frac_ref, cell_ref, layer_ref, d_ref, s_ref, acc_ref, out_ref):
-    d_ids = packed_iota(24, -192)
-    s_ids = packed_iota(4, 0)
+    d_ids = packed_iota(6, 0)
+    s_ids = packed_iota(16, 0)
     one = jnp.ones((1, 16, 128), BF16)
     zero = jnp.zeros((1, 16, 128), BF16)
     acc_ref[...] = jnp.zeros_like(acc_ref)
     per = 4
 
     def step(k, carry):
-        lefts, highs, lows = [], [], []
+        rights, highs, lows = [], [], []
         for q in range(per):
             r = k * per + q
-            d = spread_row(d_ref[pl.ds(r, 1), :])
-            s = spread_row(s_ref[pl.ds(r, 1), :])
-            lefts.append(jnp.where(d_ids == d, one, zero).reshape(384, 128))
-            mask = s_ids == s
+            mask = d_ids == spread_row(d_ref[pl.ds(r, 1), :])
+            rights.append(jnp.where(s_ids == spread_row(s_ref[pl.ds(r, 1), :]), one, zero).reshape(256, 128))
             v = val_ref[pl.ds(r, 1), :]
             fx = frac_ref[0:1, pl.ds(pl.multiple_of(r * 128, 128), 128)]
             fy = frac_ref[1:2, pl.ds(pl.multiple_of(r * 128, 128), 128)]
@@ -97,32 +93,39 @@
             for into, p in ((highs, 0), (lows, 1)):
                 into.append(
                     jnp.concatenate(
-                        [jnp.where(mask, spread_row(w[p]), zero).reshape(SLOT, 128) for w in parts],
+                        [jnp.where(mask, spread_row(w[p]), zero).reshape(96, 128) for w in parts],
                         axis=0,
                     )
                 )
-        left = jnp.concatenate(lefts, axis=1)
-        acc_ref[...] += dot_t(left, jnp.concatenate(highs, axis=1)) + dot_t(
-            left, jnp.concatenate(lows, axis=1)
+        right = jnp.concatenate(rights, axis=1)
+        acc_ref[...] += dot_t(jnp.concatenate(highs, axis=1), right) + dot_t(
+            jnp.concatenate(lows, axis=1), right
         )
         return carry
 
     lax.fori_loop(0, ROWS // per, step, 0)
+    low = lax.broadcasted_iota(jnp.int32, (32, 128), 1) < SLOT
     for c in range(CHUNKS):
-        for h in range(2):
-            out_ref[:, 2 * c + h, :] = acc_ref[c * TILES : (c + 1) * TILES, h * 128 : (h + 1) * 128]
-
-
-def place_of(tx, ty):
-    return tx // 8, (tx // 2) % 4, (tx % 2) * 2 + ty
-
-
-def partner(tx, ty, off, sign):
-    z, y, x = place_of(tx, ty)
-    z = (z + sign * (off // 16) + 8) % 8
-    y = (y + sign * ((off // 4) % 4) + 4) % 4
-    x = (x + sign * (off % 4) + 4) % 4
-    return z * 8 + y * 2 + x // 2, x % 2
+        for col in range(2):
+            plain = [acc_ref[w * 96 + c * 32 : w * 96 + c * 32 + 32, col * 128 : col * 128 + 128] for w in range(4)]
+            moved = [pltpu.roll(w, SLOT, 1) for w in plain]
+            for half in range(2):
+                at = (2 * col + half) * 32
+                for h in range(2):
+                    first, last = (plain[2 * h], moved[2 * h + 1]) if half == 0 else (moved[2 * h], plain[2 * h + 1])
+                    out_ref[at : at + 32, 2 * c + h, :] = jnp.where(low, first, last)
+
+
+def peers(tx, ty):
+    z, y, x = tx // 8, (tx // 2) % 4, (tx % 2) * 2 + ty
+    z_parts = [((z + dz) % 8) * 8 for dz in range(8)]
+
+    def pair(q):
+        px = (x + q) % 4
+        py = (y + q // 4) % 4
+        return py, px
+
+    return z_parts, pair
 
 
 def spread_block(r_ref, first, acc_ref):
@@ -176,10 +179,6 @@
         )
 
 
-def order_of(i):
-    return (i % 8) * 16 + i // 8
-
-
 def remote(src, dst, send_sem, recv_sem, where):
     return pltpu.make_async_remote_copy(
         src_ref=src, dst_ref=dst, send_sem=send_sem, recv_sem=recv_sem, device_id=where, device_id_type=MESH_ID
@@ -198,11 +197,12 @@
 
 
 def all_kernel(
-    length_ref, val_ref, frac_ref, cell_ref, layer_ref, tile_ref, ens_hbm, out_ref,
+    length_ref, val_hbm, frac_hbm, cell_hbm, layer_hbm, tile_hbm, ens_hbm, out_ref,
+    val_ref, frac_ref, cell_ref, layer_ref, tile_ref,
     d_ref, s_ref, acc_ref, sbuf, rbuf, grid_ref, ens_ref, col_ref,
     part_buf, part_got, next_buf, east_buf, east_got, north_buf, north_got, corner_buf, corner_got,
     g_ref, c_ref, f_ref, xe_buf, xe_got, ce_buf, ce_got, cc_buf, cc_got, hx_ref, hy_ref,
-    ens_sem, send_sem, recv_sem, send1, recv1, send2, recv2,
+    in_sem, ens_sem, send_sem, recv_sem, send1, recv1, send2, recv2,
 ):
     tx = lax.axis_index("tx")
     ty = lax.axis_index("ty")
@@ -214,34 +214,60 @@
     twin = 1 - mem
     barrier = pltpu.get_barrier_semaphore()
 
-    def greet(i, carry):
-        px, py = partner(tx, ty, order_of(i), 1)
+    z_parts, pair = peers(tx, ty)
+
+    def over_peers(act):
+        def some(q, steps):
+            py, px = pair(q)
+            for dz in steps:
+                act(q * 8 + dz, z_parts[dz] + py * 2 + px // 2, px % 2, px * 32 + z_parts[dz] // 2 + py)
+
+        some(0, range(1, 8))
+
+        def step(q, carry):
+            some(q, range(8))
+            return carry
+
+        lax.fori_loop(1, 16, step, 0)
+
+    def copy_in(src, dst, i):
+        copy = pltpu.make_async_copy(src, dst, in_sem.at[i])
+        copy.start()
+        return copy
+
+    tile_in = copy_in(tile_hbm, tile_ref, 0)
+    others_in = [
+        copy_in(val_hbm, val_ref, 1),
+        copy_in(frac_hbm, frac_ref, 2),
+        copy_in(cell_hbm, cell_ref, 3),
+        copy_in(layer_hbm, layer_ref, 4),
+    ]
+    ens_copy = pltpu.make_async_copy(ens_hbm, ens_ref, ens_sem)
+    ens_copy.start()
+
+    def greet(i, px, py, at):
         pl.semaphore_signal(barrier, inc=1, device_id={"tx": px, "ty": py, "mem": mem}, device_id_type=MESH_ID)
-        return carry
-
-    lax.fori_loop(1, TILES, greet, 0)
+
+    over_peers(greet)
     for px, py in ((tx, ty), (west, ty), (tx, over), (west, over)):
         pl.semaphore_signal(barrier, inc=1, device_id={"tx": px, "ty": py, "mem": twin}, device_id_type=MESH_ID)
-    ens_copy = pltpu.make_async_copy(ens_hbm, ens_ref, ens_sem)
-    ens_copy.start()
-
+    tile_in.wait()
     rank_stage(length_ref[0], tile_ref, d_ref, s_ref)
+    for copy in others_in:
+        copy.wait()
     pack_stage(val_ref, frac_ref, cell_ref, layer_ref, d_ref, s_ref, acc_ref, sbuf)
 
     pl.semaphore_wait(barrier, TILES - 1 + 4)
 
-    def message(i):
-        px, py = partner(tx, ty, order_of(i), 1)
-        return remote(
-            sbuf.at[px * 2 + py], rbuf.at[i], send_sem.at[i], recv_sem.at[i], {"tx": px, "ty": py, "mem": mem}
-        )
-
-    def send(i, carry):
-        message(i).start()
-        return carry
-
-    lax.fori_loop(1, TILES, send, 0)
-    rbuf[pl.ds(0, 1)] = sbuf[pl.ds(tx * 2 + ty, 1)]
+    def message(i, px, py, at):
+        return remote(sbuf.at[at], rbuf.at[i], send_sem.at[i], recv_sem.at[i], {"tx": px, "ty": py, "mem": mem})
+
+    def slot(i):
+        return message(i, west, ty, 0)
+
+    over_peers(lambda *peer: message(*peer).start())
+    z_own, pair_own = z_parts[0], pair(0)
+    rbuf[pl.ds(0, 1)] = sbuf[pl.ds(pair_own[1] * 32 + z_own // 2 + pair_own[0], 1)]
     edge = (1 - ty) * 127
     ens_copy.wait()
     edge_columns(ens_ref, edge, col_ref)
@@ -249,7 +275,7 @@
     grid_ref[...] = jnp.zeros_like(grid_ref)
 
     def arrive(i, carry):
-        message(i).wait_recv()
+        slot(i).wait_recv()
         return carry
 
     def gather(k, carry):
@@ -385,7 +411,7 @@
         copy.wait_send()
 
     def sent(i, carry):
-        message(i).wait_send()
+        slot(i).wait_send()
         return carry
 
     lax.fori_loop(1, TILES, sent, 0)
@@ -397,9 +423,14 @@
     out = pl.pallas_call(
         all_kernel,
         out_shape=jax.ShapeDtypeStruct((40, 32, 128), BF16),
-        in_specs=[pl.BlockSpec(memory_space=pltpu.SMEM)] + [VMEM_SPEC] * 5 + [pl.BlockSpec(memory_space=pl.ANY)],
+        in_specs=[pl.BlockSpec(memory_space=pltpu.SMEM)] + [pl.BlockSpec(memory_space=pl.ANY)] * 6,
         out_specs=VMEM_SPEC,
         scratch_shapes=[
+            pltpu.VMEM(square, F32),
+            pltpu.VMEM((2, ROWS * 128), F32),
+            pltpu.VMEM(square, jnp.int32),
+            pltpu.VMEM(square, jnp.int32),
+            pltpu.VMEM(square, jnp.int32),
             pltpu.VMEM(square, F32),
             pltpu.VMEM(square, F32),
             pltpu.VMEM((384, 256), F32),
@@ -428,6 +459,7 @@
             pltpu.VMEM((2, 2, 128), F32),
             pltpu.VMEM((2, 80, 128), F32),
             pltpu.VMEM((32, 128), F32),
+            dma((5,)),
             dma,
             dma((TILES,)),
             dma((TILES,)),

time: 64.8 us -> 54.6 us (0.84)
  Pallas kernels: 62.2 us -> 52.1 us
    pallas_call x1, Pallas kernels: 62.2 us -> 52.1 us  [body(): pl.pallas_call(all_kernel, out_shape=jax.ShapeDtypeStruct((40, 32, 128),...]
where the time goes in v3:
time: 54.6 us; the launch traced here: 54.5 us
  Pallas kernels  52.1 us (95%)
  local copies, waits for them, and re-layouts  1.72 us (3%)
  between operations  0.66 us (1%)
    pallas_call x1, Pallas kernels, body(): pl.pallas_call(all_kernel, out_shape=jax.ShapeDtypeStruct((40, 32, 128),...  52.1 us
    unnamed x1, local copies, waits for them, and re-layouts  1.72 us

profile of v3, /device:TPU:1, one launch (start us, length us, event | category | flops | bytes accessed | tf_op | source)
XLA Modules:
  0.0 54.5 jit_solution(9521256730173489166)
XLA Ops:
  0.7 52.1 %shard_map.73 = bf16[40,32,128]{2,1,0:T(8,128)(2,1)} custom-call(s32[1]{0:T(128)S(6)} %copy.9.length_ref, f32[64,128]{1,0:T(8,128)} %bitcast.8, f32[2,8192]{1,0:T(2,128)} %frac_hbm.1, s32[64,128]{1,0:T(8,128)} %bitcast.9, s32[64,128]{1,0:T(8,128)} %bitcast.10, s32[64,128]{1,0:T(8,128)} %bitcast.11, bf16[40,192,128]{2,1,0:T(8,128)(2,1)} %bitcast.6), custom_call_target="tpu_custom_call" | custom-call | tf_op jit(solution)/shard_map/pallas_call | solution.py:423
  52.7 1.7 %copy.10 = bf16[40,2,16,128]{3,2,1,0:T(8,128)(2,1)} copy(bf16[40,2,16,128]{3,2,1,0:T(8,128)(2,1)} %bitcast.7) | data formatting | bytes 655360

commit v4 on v3

--- a/solution.py
+++ b/solution.py
@@ -75,7 +75,7 @@
     one = jnp.ones((1, 16, 128), BF16)
     zero = jnp.zeros((1, 16, 128), BF16)
     acc_ref[...] = jnp.zeros_like(acc_ref)
-    per = 4
+    per = 16
 
     def step(k, carry):
         rights, highs, lows = [], [], []
@@ -260,10 +260,11 @@
     pl.semaphore_wait(barrier, TILES - 1 + 4)
 
     def message(i, px, py, at):
-        return remote(sbuf.at[at], rbuf.at[i], send_sem.at[i], recv_sem.at[i], {"tx": px, "ty": py, "mem": mem})
-
-    def slot(i):
-        return message(i, west, ty, 0)
+        return remote(sbuf.at[at], rbuf.at[i], send_sem, recv_sem.at[i // 16], {"tx": px, "ty": py, "mem": mem})
+
+    def group(k, first, count):
+        at = pl.ds(first, count)
+        return remote(sbuf.at[at], rbuf.at[at], send_sem, recv_sem.at[k], {"tx": west, "ty": ty, "mem": mem})
 
     over_peers(lambda *peer: message(*peer).start())
     z_own, pair_own = z_parts[0], pair(0)
@@ -274,16 +275,15 @@
 
     grid_ref[...] = jnp.zeros_like(grid_ref)
 
-    def arrive(i, carry):
-        slot(i).wait_recv()
-        return carry
+    group(0, 1, 15).wait_recv()
+    spread_block(rbuf, 0, grid_ref)
 
     def gather(k, carry):
-        lax.fori_loop(jnp.maximum(k * 16, 1), k * 16 + 16, arrive, 0)
+        group(k, k * 16, 16).wait_recv()
         spread_block(rbuf, k * 16, grid_ref)
         return carry
 
-    lax.fori_loop(0, 8, gather, 0)
+    lax.fori_loop(1, 8, gather, 0)
 
     row = lax.broadcasted_iota(jnp.int32, (192, 128), 0)
     x_first = (row % 16) == 0
@@ -410,11 +410,7 @@
     for copy in first:
         copy.wait_send()
 
-    def sent(i, carry):
-        slot(i).wait_send()
-        return carry
-
-    lax.fori_loop(1, TILES, sent, 0)
+    group(0, 0, TILES - 1).wait_send()
 
 
 def body(obs_value, obs_frac, obs_cell, obs_layer, obs_tile, obs_length, ensemble):
@@ -422,7 +418,7 @@
     dma = pltpu.SemaphoreType.DMA
     out = pl.pallas_call(
         all_kernel,
-        out_shape=jax.ShapeDtypeStruct((40, 32, 128), BF16),
+        out_shape=pltpu.VMEM((40, 32, 128), BF16),
         in_specs=[pl.BlockSpec(memory_space=pltpu.SMEM)] + [pl.BlockSpec(memory_space=pl.ANY)] * 6,
         out_specs=VMEM_SPEC,
         scratch_shapes=[
@@ -461,8 +457,8 @@
             pltpu.VMEM((32, 128), F32),
             dma((5,)),
             dma,
-            dma((TILES,)),
-            dma((TILES,)),
+            dma,
+            dma((8,)),
             dma((7,)),
             dma((7,)),
             dma((5,)),

time: 54.6 us -> 46.8 us (0.86)
  Pallas kernels: 52.1 us -> 45.3 us
  local copies, waits for them, and re-layouts: 1.72 us -> 0.73 us
    pallas_call x1, Pallas kernels: 52.1 us -> 45.3 us  [body(): pl.pallas_call(all_kernel, out_shape=pltpu.VMEM((40, 32, 128), BF16), in_...]
    unnamed x1, local copies, waits for them, and re-layouts: 1.72 us -> 0.73 us
where the time goes in v4:
time: 46.8 us; the launch traced here: 46.7 us
  Pallas kernels  45.3 us (97%)
  local copies, waits for them, and re-layouts  0.73 us (2%)
  between operations  0.66 us (1%)
    pallas_call x1, Pallas kernels, body(): pl.pallas_call(all_kernel, out_shape=pltpu.VMEM((40, 32, 128), BF16), in_...  45.3 us

profile of v4, /device:TPU:1, one launch (start us, length us, event | category | flops | bytes accessed | tf_op | source)
XLA Modules:
  0.0 46.7 jit_solution(10348454434139124480)
XLA Ops:
  0.7 45.3 %shard_map.73 = bf16[40,32,128]{2,1,0:T(8,128)(2,1)S(1)} custom-call(s32[1]{0:T(128)S(6)} %copy.10.length_ref, f32[64,128]{1,0:T(8,128)} %bitcast.8, f32[2,8192]{1,0:T(2,128)} %frac_hbm.1, s32[64,128]{1,0:T(8,128)} %bitcast.9, s32[64,128]{1,0:T(8,128)} %bitcast.10, s32[64,128]{1,0:T(8,128)} %bitcast.11, bf16[40,192,128]{2,1,0:T(8,128)(2,1)} %bitcast.7), custom_call_target="tpu_custom_call" | custom-call | tf_op jit(solution)/shard_map/pallas_call | solution.py:419
  46.0 0.7 %copy.9 = bf16[40,2,16,128]{3,2,1,0:T(8,128)(2,1)} copy(bf16[40,2,16,128]{3,2,1,0:T(8,128)(2,1)S(1)} %bitcast.6) | data formatting | bytes 655360

commit v5 on v4

--- a/solution.py
+++ b/solution.py
@@ -41,7 +41,7 @@
     return lax.dot_general(a, b, (((1,), (0,)), ((), ())), preferred_element_type=F32)
 
 
-def rank_stage(length, tile_ref, d_ref, s_ref):
+def rank_stage(length, z_own, tile_ref, d_ref, s_ref):
     i = lax.broadcasted_iota(jnp.int32, (128, 256), 0)
     j = lax.broadcasted_iota(jnp.int32, (128, 256), 1)
     before = jnp.where((i < j) | (j >= 128), 1.0, 0.0).astype(BF16)
@@ -62,15 +62,20 @@
             c = jnp.floor(rank * (1.0 / SLOT))
             tf = t.astype(F32)
             t4 = jnp.floor(tf * 0.25)
-            d_ref[pl.ds(r, 1), :] = jnp.where(live, c * 32.0 + t4, DEAD)
+            z = jnp.floor(t4 * 0.25)
+            e = z - z_own.astype(F32) + 6.0
+            e = e - 8.0 * jnp.floor(e * 0.125)
+            near = jnp.where(e >= 4.0, 1.0, 0.0)
+            d = near * 48.0 + c * 16.0 + (e - near * 4.0) * 4.0 + (t4 - z * 4.0)
+            d_ref[pl.ds(r, 1), :] = jnp.where(live, d, DEAD)
             s_ref[pl.ds(r, 1), :] = (tf - 4.0 * t4) * SLOT + (rank - c * SLOT)
         return offset
 
     lax.fori_loop(0, ROWS // per, step, jnp.zeros((TILES, 128), F32))
 
 
-def pack_stage(val_ref, frac_ref, cell_ref, layer_ref, d_ref, s_ref, acc_ref, out_ref):
-    d_ids = packed_iota(6, 0)
+def pack_stage(near, val_ref, frac_ref, cell_ref, layer_ref, d_ref, s_ref, acc_ref, out_ref):
+    d_ids = packed_iota(3, near * 48)
     s_ids = packed_iota(16, 0)
     one = jnp.ones((1, 16, 128), BF16)
     zero = jnp.zeros((1, 16, 128), BF16)
@@ -93,7 +98,7 @@
             for into, p in ((highs, 0), (lows, 1)):
                 into.append(
                     jnp.concatenate(
-                        [jnp.where(mask, spread_row(w[p]), zero).reshape(96, 128) for w in parts],
+                        [jnp.where(mask, spread_row(w[p]), zero).reshape(48, 128) for w in parts],
                         axis=0,
                     )
                 )
@@ -104,16 +109,16 @@
         return carry
 
     lax.fori_loop(0, ROWS // per, step, 0)
-    low = lax.broadcasted_iota(jnp.int32, (32, 128), 1) < SLOT
+    low = lax.broadcasted_iota(jnp.int32, (16, 128), 1) < SLOT
     for c in range(CHUNKS):
         for col in range(2):
-            plain = [acc_ref[w * 96 + c * 32 : w * 96 + c * 32 + 32, col * 128 : col * 128 + 128] for w in range(4)]
+            plain = [acc_ref[w * 48 + c * 16 : w * 48 + c * 16 + 16, col * 128 : col * 128 + 128] for w in range(4)]
             moved = [pltpu.roll(w, SLOT, 1) for w in plain]
             for half in range(2):
-                at = (2 * col + half) * 32
+                at = (2 * col + half) * 32 + near * 16
                 for h in range(2):
                     first, last = (plain[2 * h], moved[2 * h + 1]) if half == 0 else (moved[2 * h], plain[2 * h + 1])
-                    out_ref[at : at + 32, 2 * c + h, :] = jnp.where(low, first, last)
+                    out_ref[at : at + 16, 2 * c + h, :] = jnp.where(low, first, last)
 
 
 def peers(tx, ty):
@@ -196,10 +201,21 @@
     out_ref[...] = total
 
 
+def edge_rows(ens_ref, out_ref):
+    def step(m, carry):
+        for k in range(12):
+            block = ens_ref[m, k * 16 : k * 16 + 16, :].astype(F32)
+            out_ref[0, k, pl.ds(m, 1), :] = block[0:1, :]
+            out_ref[1, k, pl.ds(m, 1), :] = block[15:16, :]
+        return carry
+
+    lax.fori_loop(0, 40, step, 0)
+
+
 def all_kernel(
     length_ref, val_hbm, frac_hbm, cell_hbm, layer_hbm, tile_hbm, ens_hbm, out_ref,
     val_ref, frac_ref, cell_ref, layer_ref, tile_ref,
-    d_ref, s_ref, acc_ref, sbuf, rbuf, grid_ref, ens_ref, col_ref,
+    d_ref, s_ref, acc_ref, sbuf, rbuf, grid_ref, ens_ref, col_ref, rows_ref,
     part_buf, part_got, next_buf, east_buf, east_got, north_buf, north_got, corner_buf, corner_got,
     g_ref, c_ref, f_ref, xe_buf, xe_got, ce_buf, ce_got, cc_buf, cc_got, hx_ref, hy_ref,
     in_sem, ens_sem, send_sem, recv_sem, send1, recv1, send2, recv2,
@@ -216,16 +232,20 @@
 
     z_parts, pair = peers(tx, ty)
 
-    def over_peers(act):
-        def some(q, steps):
+    def over_peers(act, near):
+        steps = (0, 1, 7, 6) if near else (4, 3, 5, 2)
+
+        def some(q, first):
             py, px = pair(q)
-            for dz in steps:
-                act(q * 8 + dz, z_parts[dz] + py * 2 + px // 2, px % 2, px * 32 + z_parts[dz] // 2 + py)
-
-        some(0, range(1, 8))
+            for n in range(first, 4):
+                dz = steps[n]
+                place = px * 32 + (dz + 6) % 8 * 4 + py
+                act(near * 64 + q * 4 + n, z_parts[dz] + py * 2 + px // 2, px % 2, place)
+
+        some(0, near)
 
         def step(q, carry):
-            some(q, range(8))
+            some(q, 0)
             return carry
 
         lax.fori_loop(1, 16, step, 0)
@@ -248,14 +268,16 @@
     def greet(i, px, py, at):
         pl.semaphore_signal(barrier, inc=1, device_id={"tx": px, "ty": py, "mem": mem}, device_id_type=MESH_ID)
 
-    over_peers(greet)
+    over_peers(greet, 0)
+    over_peers(greet, 1)
     for px, py in ((tx, ty), (west, ty), (tx, over), (west, over)):
         pl.semaphore_signal(barrier, inc=1, device_id={"tx": px, "ty": py, "mem": twin}, device_id_type=MESH_ID)
     tile_in.wait()
-    rank_stage(length_ref[0], tile_ref, d_ref, s_ref)
+    rank_stage(length_ref[0], tx // 8, tile_ref, d_ref, s_ref)
     for copy in others_in:
         copy.wait()
-    pack_stage(val_ref, frac_ref, cell_ref, layer_ref, d_ref, s_ref, acc_ref, sbuf)
+    packing = (val_ref, frac_ref, cell_ref, layer_ref, d_ref, s_ref, acc_ref, sbuf)
+    pack_stage(0, *packing)
 
     pl.semaphore_wait(barrier, TILES - 1 + 4)
 
@@ -266,24 +288,27 @@
         at = pl.ds(first, count)
         return remote(sbuf.at[at], rbuf.at[at], send_sem, recv_sem.at[k], {"tx": west, "ty": ty, "mem": mem})
 
-    over_peers(lambda *peer: message(*peer).start())
-    z_own, pair_own = z_parts[0], pair(0)
-    rbuf[pl.ds(0, 1)] = sbuf[pl.ds(pair_own[1] * 32 + z_own // 2 + pair_own[0], 1)]
+    over_peers(lambda *peer: message(*peer).start(), 0)
+    pack_stage(1, *packing)
+    over_peers(lambda *peer: message(*peer).start(), 1)
+    py, px = pair(0)
+    rbuf[pl.ds(64, 1)] = sbuf[pl.ds(px * 32 + 24 + py, 1)]
     edge = (1 - ty) * 127
     ens_copy.wait()
     edge_columns(ens_ref, edge, col_ref)
+    edge_rows(ens_ref, rows_ref)
 
     grid_ref[...] = jnp.zeros_like(grid_ref)
-
-    group(0, 1, 15).wait_recv()
-    spread_block(rbuf, 0, grid_ref)
 
     def gather(k, carry):
         group(k, k * 16, 16).wait_recv()
         spread_block(rbuf, k * 16, grid_ref)
         return carry
 
-    lax.fori_loop(1, 8, gather, 0)
+    lax.fori_loop(0, 4, gather, 0)
+    group(4, 65, 15).wait_recv()
+    spread_block(rbuf, 64, grid_ref)
+    lax.fori_loop(5, 8, gather, 0)
 
     row = lax.broadcasted_iota(jnp.int32, (192, 128), 0)
     x_first = (row % 16) == 0
@@ -324,6 +349,22 @@
     wall = jnp.broadcast_to(wall[:, None, :], (12, 16, 128)).reshape(192, 128)
     g = part_buf[...] + part_got[...] + rims[0:192, :] + jnp.where(x_first, wall, 0.0)
     g_ref[...] = g
+    for n in range(2):
+        for v in range(2):
+            total = jnp.zeros((40, 128), F32)
+            for t in range(6):
+                at = (t * 2 + v) * 16 + 15 * n
+                total = total + rows_ref[n, t * 2 + v] * g[at : at + 1, :]
+            xe_buf[n, v * 40 : v * 40 + 40, :] = total
+    second = [
+        remote(xe_buf.at[0], xe_got.at[1], send2.at[0], recv2.at[1], {"tx": west, "ty": ty, "mem": mem}),
+        remote(xe_buf.at[1], xe_got.at[0], send2.at[1], recv2.at[0], {"tx": east, "ty": ty, "mem": mem}),
+        remote(ce_buf, ce_got, send2.at[2], recv2.at[2], {"tx": tx, "ty": over, "mem": mem}),
+        remote(cc_buf.at[0], cc_got.at[1], send2.at[3], recv2.at[4], {"tx": west, "ty": over, "mem": mem}),
+        remote(cc_buf.at[1], cc_got.at[0], send2.at[4], recv2.at[3], {"tx": east, "ty": over, "mem": mem}),
+    ]
+    second[0].start()
+    second[1].start()
     gcol = jnp.sum(jnp.where(lane192 == edge, g, 0.0), axis=1, keepdims=True)
     ce = jnp.zeros((32, 128), F32)
     for t in range(6):
@@ -333,6 +374,9 @@
         cc_buf[0, v : v + 1, :] = ce[v * 16 : v * 16 + 1, :]
         cc_buf[1, v : v + 1, :] = ce[v * 16 + 15 : v * 16 + 16, :]
 
+    for copy in second[2:]:
+        copy.start()
+
     def contract(m, carry):
         total = jnp.zeros((32, 128), F32)
         for t in range(6):
@@ -341,19 +385,6 @@
         return carry
 
     lax.fori_loop(0, 40, contract, 0)
-    xe_buf[0] = c_ref[pl.ds(0, 80, stride=16), :]
-    xe_buf[1] = c_ref[pl.ds(15, 80, stride=16), :]
-
-    second = [
-        remote(xe_buf.at[0], xe_got.at[1], send2.at[0], recv2.at[1], {"tx": west, "ty": ty, "mem": mem}),
-        remote(xe_buf.at[1], xe_got.at[0], send2.at[1], recv2.at[0], {"tx": east, "ty": ty, "mem": mem}),
-        remote(ce_buf, ce_got, send2.at[2], recv2.at[2], {"tx": tx, "ty": over, "mem": mem}),
-        remote(cc_buf.at[0], cc_got.at[1], send2.at[3], recv2.at[4], {"tx": west, "ty": over, "mem": mem}),
-        remote(cc_buf.at[1], cc_got.at[0], send2.at[4], recv2.at[3], {"tx": east, "ty": over, "mem": mem}),
-    ]
-    for copy in second:
-        copy.start()
-
     row32 = lax.broadcasted_iota(jnp.int32, (32, 128), 0) % 16
     lane32 = lax.broadcasted_iota(jnp.int32, (32, 128), 1)
 
@@ -398,8 +429,8 @@
         f = f_ref[at, :] + jnp.where(lane32 == edge, pltpu.roll(hy_ref[...], lax.rem(edge - m + 128, 128), 1), 0.0)
         low, high = [], []
         for v in range(2):
-            low.append(jnp.broadcast_to(hx_ref[0, pl.ds(2 * m + v, 1), :], (16, 128)))
-            high.append(jnp.broadcast_to(hx_ref[1, pl.ds(2 * m + v, 1), :], (16, 128)))
+            low.append(jnp.broadcast_to(hx_ref[0, pl.ds(v * 40 + m, 1), :], (16, 128)))
+            high.append(jnp.broadcast_to(hx_ref[1, pl.ds(v * 40 + m, 1), :], (16, 128)))
         f = f + jnp.where(row32 == 0, jnp.concatenate(low, axis=0), 0.0)
         f = f + jnp.where(row32 == 15, jnp.concatenate(high, axis=0), 0.0)
         out_ref[m] = f.astype(BF16)
@@ -429,12 +460,13 @@
             pltpu.VMEM(square, jnp.int32),
             pltpu.VMEM(square, F32),
             pltpu.VMEM(square, F32),
-            pltpu.VMEM((384, 256), F32),
+            pltpu.VMEM((192, 256), F32),
             pltpu.VMEM((TILES, 6, 128), F32),
             pltpu.VMEM((TILES, 6, 128), F32),
             pltpu.VMEM((272, 192), F32),
             pltpu.VMEM((40, 192, 128), BF16),
             pltpu.VMEM((192, 128), F32),
+            pltpu.VMEM((2, 12, 40, 128), F32),
             pltpu.VMEM((192, 128), F32),
             pltpu.VMEM((192, 128), F32),
             pltpu.VMEM((192, 128), F32),

time: 46.8 us -> 49.1 us (1.049)
  Pallas kernels: 45.3 us -> 47.6 us
    pallas_call x1, Pallas kernels: 45.3 us -> 47.6 us  [body(): pl.pallas_call(all_kernel, out_shape=pltpu.VMEM((40, 32, 128), BF16), in_...]
where the time goes in v5:
time: 49.1 us; the launch traced here: 49 us
  Pallas kernels  47.6 us (97%)
  local copies, waits for them, and re-layouts  0.73 us (1%)
  between operations  0.66 us (1%)
    pallas_call x1, Pallas kernels, body(): pl.pallas_call(all_kernel, out_shape=pltpu.VMEM((40, 32, 128), BF16), in_...  47.6 us

profile of v5, /device:TPU:1, one launch (start us, length us, event | category | flops | bytes accessed | tf_op | source)
XLA Modules:
  0.0 49.0 jit_solution(7683730076157718559)
XLA Ops:
  0.7 47.6 %shard_map.73 = bf16[40,32,128]{2,1,0:T(8,128)(2,1)S(1)} custom-call(s32[1]{0:T(128)S(6)} %copy.10.length_ref, f32[64,128]{1,0:T(8,128)} %bitcast.8, f32[2,8192]{1,0:T(2,128)} %frac_hbm.1, s32[64,128]{1,0:T(8,128)} %bitcast.9, s32[64,128]{1,0:T(8,128)} %bitcast.10, s32[64,128]{1,0:T(8,128)} %bitcast.11, bf16[40,192,128]{2,1,0:T(8,128)(2,1)} %bitcast.7), custom_call_target="tpu_custom_call" | custom-call | tf_op jit(solution)/shard_map/pallas_call | solution.py:450
  48.3 0.7 %copy.9 = bf16[40,2,16,128]{3,2,1,0:T(8,128)(2,1)} copy(bf16[40,2,16,128]{3,2,1,0:T(8,128)(2,1)S(1)} %bitcast.6) | data formatting | bytes 655360

commit v6 on v5

--- a/solution.py
+++ b/solution.py
@@ -102,10 +102,13 @@
                         axis=0,
                     )
                 )
-        right = jnp.concatenate(rights, axis=1)
-        acc_ref[...] += dot_t(jnp.concatenate(highs, axis=1), right) + dot_t(
-            jnp.concatenate(lows, axis=1), right
-        )
+        total = jnp.zeros((384, 256), F32)
+        for part in (slice(0, per // 2), slice(per // 2, per)):
+            left = jnp.concatenate(
+                [jnp.concatenate(highs[part], axis=1), jnp.concatenate(lows[part], axis=1)], axis=0
+            )
+            total = total + dot_t(left, jnp.concatenate(rights[part], axis=1))
+        acc_ref[...] += total[:192] + total[192:]
         return carry
 
     lax.fori_loop(0, ROWS // per, step, 0)
@@ -233,22 +236,21 @@
     z_parts, pair = peers(tx, ty)
 
     def over_peers(act, near):
-        steps = (0, 1, 7, 6) if near else (4, 3, 5, 2)
-
-        def some(q, first):
+        steps = (1, 7, 6, 0) if near else (4, 3, 5, 2)
+
+        def some(q, count):
             py, px = pair(q)
-            for n in range(first, 4):
+            for n in range(count):
                 dz = steps[n]
                 place = px * 32 + (dz + 6) % 8 * 4 + py
-                act(near * 64 + q * 4 + n, z_parts[dz] + py * 2 + px // 2, px % 2, place)
-
-        some(0, near)
-
-        def step(q, carry):
-            some(q, 0)
+                act(near * 4 + (15 - q) // 4, (15 - q) % 4 * 4 + n, z_parts[dz] + py * 2 + px // 2, px % 2, place)
+
+        def step(i, carry):
+            some(15 - i, 4)
             return carry
 
-        lax.fori_loop(1, 16, step, 0)
+        lax.fori_loop(0, 15, step, 0)
+        some(0, 4 - near)
 
     def copy_in(src, dst, i):
         copy = pltpu.make_async_copy(src, dst, in_sem.at[i])
@@ -265,7 +267,7 @@
     ens_copy = pltpu.make_async_copy(ens_hbm, ens_ref, ens_sem)
     ens_copy.start()
 
-    def greet(i, px, py, at):
+    def greet(k, n, px, py, at):
         pl.semaphore_signal(barrier, inc=1, device_id={"tx": px, "ty": py, "mem": mem}, device_id_type=MESH_ID)
 
     over_peers(greet, 0)
@@ -281,18 +283,19 @@
 
     pl.semaphore_wait(barrier, TILES - 1 + 4)
 
-    def message(i, px, py, at):
-        return remote(sbuf.at[at], rbuf.at[i], send_sem, recv_sem.at[i // 16], {"tx": px, "ty": py, "mem": mem})
-
-    def group(k, first, count):
+    def message(k, n, px, py, at):
+        there = {"tx": px, "ty": py, "mem": mem}
+        return remote(sbuf.at[at], rbuf.at[k * 16 + n], send_sem, recv_sem.at[k * 2 + n // 15], there)
+
+    def group(sem, first, count):
         at = pl.ds(first, count)
-        return remote(sbuf.at[at], rbuf.at[at], send_sem, recv_sem.at[k], {"tx": west, "ty": ty, "mem": mem})
+        return remote(sbuf.at[at], rbuf.at[at], send_sem, sem, {"tx": west, "ty": ty, "mem": mem})
 
     over_peers(lambda *peer: message(*peer).start(), 0)
     pack_stage(1, *packing)
     over_peers(lambda *peer: message(*peer).start(), 1)
     py, px = pair(0)
-    rbuf[pl.ds(64, 1)] = sbuf[pl.ds(px * 32 + 24 + py, 1)]
+    rbuf[pl.ds(127, 1)] = sbuf[pl.ds(px * 32 + 24 + py, 1)]
     edge = (1 - ty) * 127
     ens_copy.wait()
     edge_columns(ens_ref, edge, col_ref)
@@ -301,14 +304,16 @@
     grid_ref[...] = jnp.zeros_like(grid_ref)
 
     def gather(k, carry):
-        group(k, k * 16, 16).wait_recv()
+        group(recv_sem.at[k * 2], k * 16, 15).wait_recv()
+
+        @pl.when(k < 7)
+        def _():
+            group(recv_sem.at[k * 2 + 1], k * 16 + 15, 1).wait_recv()
+
         spread_block(rbuf, k * 16, grid_ref)
         return carry
 
-    lax.fori_loop(0, 4, gather, 0)
-    group(4, 65, 15).wait_recv()
-    spread_block(rbuf, 64, grid_ref)
-    lax.fori_loop(5, 8, gather, 0)
+    lax.fori_loop(0, 8, gather, 0)
 
     row = lax.broadcasted_iota(jnp.int32, (192, 128), 0)
     x_first = (row % 16) == 0
@@ -377,20 +382,19 @@
     for copy in second[2:]:
         copy.start()
 
-    def contract(m, carry):
-        total = jnp.zeros((32, 128), F32)
-        for t in range(6):
-            total = total + ens_ref[m, t * 32 : t * 32 + 32, :].astype(F32) * g_ref[t * 32 : t * 32 + 32, :]
-        c_ref[pl.ds(pl.multiple_of(m * 32, 32), 32), :] = total
+    def contract(b, carry):
+        for m in range(4):
+            total = jnp.zeros((32, 128), F32)
+            for t in range(6):
+                total = total + ens_ref[b * 4 + m, t * 32 : t * 32 + 32, :].astype(F32) * g_ref[t * 32 : t * 32 + 32, :]
+            c_ref[pl.ds(pl.multiple_of(b * 128 + m * 32, 32), 32), :] = total
         return carry
 
-    lax.fori_loop(0, 40, contract, 0)
-    row32 = lax.broadcasted_iota(jnp.int32, (32, 128), 0) % 16
-    lane32 = lax.broadcasted_iota(jnp.int32, (32, 128), 1)
-
+    lax.fori_loop(0, 10, contract, 0)
     def along_x(c):
-        up = jnp.where(row32 == 0, 0.0, pltpu.roll(c, 1, 0))
-        down = jnp.where(row32 == 15, 0.0, pltpu.roll(c, 31, 0))
+        x = lax.broadcasted_iota(jnp.int32, c.shape, 0) % 16
+        up = jnp.where(x == 0, 0.0, pltpu.roll(c, 1, 0))
+        down = jnp.where(x == 15, 0.0, pltpu.roll(c, c.shape[0] - 1, 0))
         return 0.5 * c + 0.25 * (up + down)
 
     def along_y(c, lane):
@@ -398,12 +402,15 @@
         right = jnp.where(lane == 127, 0.0, pltpu.roll(c, 127, 1))
         return 0.5 * c + 0.25 * (left + right)
 
-    def inside(m, carry):
-        at = pl.ds(pl.multiple_of(m * 32, 32), 32)
-        f_ref[at, :] = along_y(along_x(c_ref[at, :]), lane32)
+    lane256 = lax.broadcasted_iota(jnp.int32, (256, 128), 1)
+    x256 = lax.broadcasted_iota(jnp.int32, (256, 128), 0) % 16
+
+    def inside(b, carry):
+        at = pl.ds(pl.multiple_of(b * 256, 256), 256)
+        f_ref[at, :] = along_y(along_x(c_ref[at, :]), lane256)
         return carry
 
-    lax.fori_loop(0, 40, inside, 0)
+    lax.fori_loop(0, 5, inside, 0)
 
     for copy in second:
         copy.wait_send()
@@ -424,24 +431,26 @@
         side = side + jnp.where(here == v * 16, before, 0.0) + jnp.where(here == v * 16 + 15, behind, 0.0)
     hy_ref[...] = side * 0.25
 
-    def finish(m, carry):
-        at = pl.ds(pl.multiple_of(m * 32, 32), 32)
-        f = f_ref[at, :] + jnp.where(lane32 == edge, pltpu.roll(hy_ref[...], lax.rem(edge - m + 128, 128), 1), 0.0)
-        low, high = [], []
-        for v in range(2):
-            low.append(jnp.broadcast_to(hx_ref[0, pl.ds(v * 40 + m, 1), :], (16, 128)))
-            high.append(jnp.broadcast_to(hx_ref[1, pl.ds(v * 40 + m, 1), :], (16, 128)))
-        f = f + jnp.where(row32 == 0, jnp.concatenate(low, axis=0), 0.0)
-        f = f + jnp.where(row32 == 15, jnp.concatenate(high, axis=0), 0.0)
-        out_ref[m] = f.astype(BF16)
+    def finish(b, carry):
+        at = pl.ds(pl.multiple_of(b * 256, 256), 256)
+        side_parts, low, high = [], [], []
+        for m in range(8):
+            side_parts.append(pltpu.roll(hy_ref[...], lax.rem(edge - (b * 8 + m) + 128, 128), 1))
+            for v in range(2):
+                low.append(jnp.broadcast_to(hx_ref[0, pl.ds(v * 40 + b * 8 + m, 1), :], (16, 128)))
+                high.append(jnp.broadcast_to(hx_ref[1, pl.ds(v * 40 + b * 8 + m, 1), :], (16, 128)))
+        f = f_ref[at, :] + jnp.where(lane256 == edge, jnp.concatenate(side_parts, axis=0), 0.0)
+        f = f + jnp.where(x256 == 0, jnp.concatenate(low, axis=0), 0.0)
+        f = f + jnp.where(x256 == 15, jnp.concatenate(high, axis=0), 0.0)
+        out_ref[pl.ds(b * 8, 8)] = f.reshape(8, 32, 128).astype(BF16)
         return carry
 
-    lax.fori_loop(0, 40, finish, 0)
+    lax.fori_loop(0, 5, finish, 0)
 
     for copy in first:
         copy.wait_send()
 
-    group(0, 0, TILES - 1).wait_send()
+    group(recv_sem.at[0], 0, TILES - 1).wait_send()
 
 
 def body(obs_value, obs_frac, obs_cell, obs_layer, obs_tile, obs_length, ensemble):
@@ -490,7 +499,7 @@
             dma((5,)),
             dma,
             dma,
-            dma((8,)),
+            dma((16,)),
             dma((7,)),
             dma((7,)),
             dma((5,)),

time: 49.1 us -> 44 us (0.90)
  Pallas kernels: 47.6 us -> 42.5 us
    pallas_call x1, Pallas kernels: 47.6 us -> 42.5 us  [body(): pl.pallas_call(all_kernel, out_shape=pltpu.VMEM((40, 32, 128), BF16), in_...]
where the time goes in v6:
time: 44 us; the launch traced here: 43.9 us
  Pallas kernels  42.5 us (97%)
  local copies, waits for them, and re-layouts  0.73 us (2%)
  between operations  0.66 us (2%)
    pallas_call x1, Pallas kernels, body(): pl.pallas_call(all_kernel, out_shape=pltpu.VMEM((40, 32, 128), BF16), in_...  42.5 us

profile of v6, /device:TPU:1, one launch (start us, length us, event | category | flops | bytes accessed | tf_op | source)
XLA Modules:
  0.0 43.9 jit_solution(17330582539329669289)
XLA Ops:
  0.7 42.5 %shard_map.73 = bf16[40,32,128]{2,1,0:T(8,128)(2,1)S(1)} custom-call(s32[1]{0:T(128)S(6)} %copy.10.length_ref, f32[64,128]{1,0:T(8,128)} %bitcast.8, f32[2,8192]{1,0:T(2,128)} %frac_hbm.1, s32[64,128]{1,0:T(8,128)} %bitcast.9, s32[64,128]{1,0:T(8,128)} %bitcast.10, s32[64,128]{1,0:T(8,128)} %bitcast.11, bf16[40,192,128]{2,1,0:T(8,128)(2,1)} %bitcast.7), custom_call_target="tpu_custom_call" | custom-call | tf_op jit(solution)/shard_map/pallas_call | solution.py:459
  43.2 0.7 %copy.9 = bf16[40,2,16,128]{3,2,1,0:T(8,128)(2,1)} copy(bf16[40,2,16,128]{3,2,1,0:T(8,128)(2,1)S(1)} %bitcast.6) | data formatting | bytes 655360

commit v7 on v6

--- a/solution.py
+++ b/solution.py
@@ -243,7 +243,7 @@
             for n in range(count):
                 dz = steps[n]
                 place = px * 32 + (dz + 6) % 8 * 4 + py
-                act(near * 4 + (15 - q) // 4, (15 - q) % 4 * 4 + n, z_parts[dz] + py * 2 + px // 2, px % 2, place)
+                act(4 - near * 4 + (15 - q) // 4, (15 - q) % 4 * 4 + n, z_parts[dz] + py * 2 + px // 2, px % 2, place)
 
         def step(i, carry):
             some(15 - i, 4)
@@ -279,7 +279,7 @@
     for copy in others_in:
         copy.wait()
     packing = (val_ref, frac_ref, cell_ref, layer_ref, d_ref, s_ref, acc_ref, sbuf)
-    pack_stage(0, *packing)
+    pack_stage(1, *packing)
 
     pl.semaphore_wait(barrier, TILES - 1 + 4)
 
@@ -291,22 +291,19 @@
         at = pl.ds(first, count)
         return remote(sbuf.at[at], rbuf.at[at], send_sem, sem, {"tx": west, "ty": ty, "mem": mem})
 
+    over_peers(lambda *peer: message(*peer).start(), 1)
+    pack_stage(0, *packing)
     over_peers(lambda *peer: message(*peer).start(), 0)
-    pack_stage(1, *packing)
-    over_peers(lambda *peer: message(*peer).start(), 1)
     py, px = pair(0)
-    rbuf[pl.ds(127, 1)] = sbuf[pl.ds(px * 32 + 24 + py, 1)]
+    rbuf[pl.ds(63, 1)] = sbuf[pl.ds(px * 32 + 24 + py, 1)]
     edge = (1 - ty) * 127
-    ens_copy.wait()
-    edge_columns(ens_ref, edge, col_ref)
-    edge_rows(ens_ref, rows_ref)
 
     grid_ref[...] = jnp.zeros_like(grid_ref)
 
     def gather(k, carry):
         group(recv_sem.at[k * 2], k * 16, 15).wait_recv()
 
-        @pl.when(k < 7)
+        @pl.when(k != 3)
         def _():
             group(recv_sem.at[k * 2 + 1], k * 16 + 15, 1).wait_recv()
 
@@ -340,6 +337,9 @@
         first.append(remote(corner_buf, corner_got.at[mem], send1.at[5 + j], recv1.at[5 + mem], {"tx": east, "ty": over, "mem": j}))
     for copy in first:
         copy.start()
+    ens_copy.wait()
+    edge_columns(ens_ref, edge, col_ref)
+    edge_rows(ens_ref, rows_ref)
     remote(part_buf, part_got, send1.at[0], recv1.at[0], {"tx": tx, "ty": ty, "mem": twin}).wait_recv()
     for j in range(2):
         remote(east_buf, east_got.at[j], send1.at[1 + j], recv1.at[1 + j], {"tx": east, "ty": ty, "mem": j}).wait_recv()

time: 44 us -> 43 us (0.977)
  Pallas kernels: 42.5 us -> 41.5 us
    pallas_call x1, Pallas kernels: 42.5 us -> 41.5 us  [body(): pl.pallas_call(all_kernel, out_shape=pltpu.VMEM((40, 32, 128), BF16), in_...]
where the time goes in v7:
time: 43 us; the launch traced here: 42.9 us
  Pallas kernels  41.5 us (97%)
  local copies, waits for them, and re-layouts  0.73 us (2%)
  between operations  0.66 us (2%)
    pallas_call x1, Pallas kernels, body(): pl.pallas_call(all_kernel, out_shape=pltpu.VMEM((40, 32, 128), BF16), in_...  41.5 us

profile of v7, /device:TPU:1, one launch (start us, length us, event | category | flops | bytes accessed | tf_op | source)
XLA Modules:
  0.0 42.9 jit_solution(6743295665132791119)
XLA Ops:
  0.7 41.5 %shard_map.73 = bf16[40,32,128]{2,1,0:T(8,128)(2,1)S(1)} custom-call(s32[1]{0:T(128)S(6)} %copy.10.length_ref, f32[64,128]{1,0:T(8,128)} %bitcast.8, f32[2,8192]{1,0:T(2,128)} %frac_hbm.1, s32[64,128]{1,0:T(8,128)} %bitcast.9, s32[64,128]{1,0:T(8,128)} %bitcast.10, s32[64,128]{1,0:T(8,128)} %bitcast.11, bf16[40,192,128]{2,1,0:T(8,128)(2,1)} %bitcast.7), custom_call_target="tpu_custom_call" | custom-call | tf_op jit(solution)/shard_map/pallas_call | solution.py:459
  42.1 0.7 %copy.9 = bf16[40,2,16,128]{3,2,1,0:T(8,128)(2,1)} copy(bf16[40,2,16,128]{3,2,1,0:T(8,128)(2,1)S(1)} %bitcast.6) | data formatting | bytes 655360

commit v8 on v7

--- a/solution.py
+++ b/solution.py
@@ -47,7 +47,7 @@
     before = jnp.where((i < j) | (j >= 128), 1.0, 0.0).astype(BF16)
     tiles_id = lax.broadcasted_iota(jnp.int32, (TILES, 128), 0)
     lane = lax.broadcasted_iota(jnp.int32, (1, 128), 1)
-    per = 4
+    per = 8
 
     def step(k, offset):
         for q in range(per):
@@ -219,7 +219,7 @@
     length_ref, val_hbm, frac_hbm, cell_hbm, layer_hbm, tile_hbm, ens_hbm, out_ref,
     val_ref, frac_ref, cell_ref, layer_ref, tile_ref,
     d_ref, s_ref, acc_ref, sbuf, rbuf, grid_ref, ens_ref, col_ref, rows_ref,
-    part_buf, part_got, next_buf, east_buf, east_got, north_buf, north_got, corner_buf, corner_got,
+    part_buf, part_got, east_buf, east_got, north_buf, north_got, corner_buf, corner_got,
     g_ref, c_ref, f_ref, xe_buf, xe_got, ce_buf, ce_got, cc_buf, cc_got, hx_ref, hy_ref,
     in_sem, ens_sem, send_sem, recv_sem, send1, recv1, send2, recv2,
 ):
@@ -320,8 +320,8 @@
     after = grid_ref[128:256, :].T
     mine = grid_ref[0:128, :].T + jnp.where(x_first, 0.0, pltpu.roll(after, 1, 0))
     part_buf[...] = mine
-    next_buf[...] = after
-    east_buf[...] = next_buf[pl.ds(15, 12, stride=16), :]
+    for k in range(12):
+        east_buf[k : k + 1, :] = after[k * 16 + 15 : k * 16 + 16, :]
     pad = jnp.zeros((8, 64), F32)
     rim0 = jnp.concatenate([jnp.broadcast_to(grid_ref[256:257, :], (8, 192)), pad], axis=1)
     rim1 = jnp.concatenate([jnp.broadcast_to(grid_ref[257:258, :], (8, 192)), pad], axis=1)
@@ -335,7 +335,7 @@
         first.append(remote(east_buf, east_got.at[mem], send1.at[1 + j], recv1.at[1 + mem], {"tx": east, "ty": ty, "mem": j}))
         first.append(remote(north_buf, north_got.at[mem], send1.at[3 + j], recv1.at[3 + mem], {"tx": tx, "ty": over, "mem": j}))
         first.append(remote(corner_buf, corner_got.at[mem], send1.at[5 + j], recv1.at[5 + mem], {"tx": east, "ty": over, "mem": j}))
-    for copy in first:
+    for copy in first[1:] + first[:1]:
         copy.start()
     ens_copy.wait()
     edge_columns(ens_ref, edge, col_ref)
@@ -478,7 +478,6 @@
             pltpu.VMEM((2, 12, 40, 128), F32),
             pltpu.VMEM((192, 128), F32),
             pltpu.VMEM((192, 128), F32),
-            pltpu.VMEM((192, 128), F32),
             pltpu.VMEM((12, 128), F32),
             pltpu.VMEM((2, 12, 128), F32),
             pltpu.VMEM((8, 256), F32),

time: 43 us -> 41.7 us (0.970)
  Pallas kernels: 41.5 us -> 40.1 us
    pallas_call x1, Pallas kernels: 41.5 us -> 40.1 us  [body(): pl.pallas_call(all_kernel, out_shape=pltpu.VMEM((40, 32, 128), BF16), in_...]
where the time goes in v8:
time: 41.7 us; the launch traced here: 41.5 us
  Pallas kernels  40.1 us (96%)
  local copies, waits for them, and re-layouts  0.73 us (2%)
  between operations  0.66 us (2%)
    pallas_call x1, Pallas kernels, body(): pl.pallas_call(all_kernel, out_shape=pltpu.VMEM((40, 32, 128), BF16), in_...  40.1 us

profile of v8, /device:TPU:1, one launch (start us, length us, event | category | flops | bytes accessed | tf_op | source)
XLA Modules:
  0.0 41.5 jit_solution(9878799860582000006)
XLA Ops:
  0.7 40.1 %shard_map.73 = bf16[40,32,128]{2,1,0:T(8,128)(2,1)S(1)} custom-call(s32[1]{0:T(128)S(6)} %copy.10.length_ref, f32[64,128]{1,0:T(8,128)} %bitcast.8, f32[2,8192]{1,0:T(2,128)} %frac_hbm.1, s32[64,128]{1,0:T(8,128)} %bitcast.9, s32[64,128]{1,0:T(8,128)} %bitcast.10, s32[64,128]{1,0:T(8,128)} %bitcast.11, bf16[40,192,128]{2,1,0:T(8,128)(2,1)} %bitcast.7), custom_call_target="tpu_custom_call" | custom-call | tf_op jit(solution)/shard_map/pallas_call | solution.py:459
  40.8 0.7 %copy.9 = bf16[40,2,16,128]{3,2,1,0:T(8,128)(2,1)} copy(bf16[40,2,16,128]{3,2,1,0:T(8,128)(2,1)S(1)} %bitcast.6) | data formatting | bytes 655360
